TPU v7x, 16 devices: a whole 2x2x2 slice. The times are simulated.
16 devices in a mesh: data: 16 (over z, y, x, core).
Axes of the slice: x: 2, y: 2, z: 2, core: 2. Of those that a mesh axis runs over, the one named last changes fastest.
Arguments:
- x_in: bfloat16 [128, 48, 512], P('data')
- targets: int32 [128, 48], P('data')
- w_lstm: bfloat16 [8, 1024, 2048], replicated
- b_lstm: float32 [8, 2048], replicated
- w_vocab: bfloat16 [512, 32000], replicated
Outputs:
- output 1: float32 [8, 1024, 2048], replicated
- output 2: float32 [8, 2048], replicated
- output 3: float32 [512, 32000], replicated
- output 4: float32 [128, 48, 512], P('data')
All inputs are finite; a program needn't handle non-finite values.
Results may differ from a plain program's by a relative error of at most 0.00726.
Values are sent between devices in bfloat16 or wider.
A program may use at most 1 GiB of HBM per device.

v0:
```python
import functools

import jax
import jax.numpy as jnp
from jax import lax
from jax.experimental import pallas as pl
from jax.experimental.pallas import tpu as pltpu
from jax.sharding import PartitionSpec as P

T = 48
R = 8
S = 8
Q = S * R
H = 512
HB = 256
G4 = 4 * H
L = 8
V = 32000
LANE = 128
NDEV = 16
CH = 4
NR = 6
PIECES = ((0, 0, 256), (256, 384, 256), (512, 384, 128))
F32 = jnp.float32
BF16 = jnp.bfloat16
MESH = pl.DeviceIdType.MESH
MIB = 1024 * 1024
ANY = pl.BlockSpec(memory_space=pl.ANY)
VMEM = pl.BlockSpec(memory_space=pltpu.VMEM)
HBM = pl.BlockSpec(memory_space=pltpu.HBM)
DMA = pltpu.SemaphoreType.DMA


def dot(a, b):
    return jnp.dot(a, b, preferred_element_type=F32)


def dot_tt(a, b):
    return lax.dot_general(a, b, (((1,), (1,)), ((), ())), preferred_element_type=F32)


def gray(k):
    chip, core = k // 2, k % 2
    hi, lo = chip // 2, chip % 2
    return 2 * (chip + hi - 2 * hi * lo) + core


LAST = gray(S - 1)


def place():
    me = lax.axis_index("data")
    index = lax.rem(me, S)
    return me - index, index, gray(index)


def plane_signal(base, index):
    barrier = pltpu.get_barrier_semaphore()
    for i in range(1, S):
        pl.semaphore_signal(barrier, inc=1, device_id=(base + lax.rem(index + i, S),), device_id_type=MESH)


def plane_wait():
    pl.semaphore_wait(pltpu.get_barrier_semaphore(), S - 1)


def rows_of(v):
    return v.reshape(Q, v.shape[-1])


def groups_of(v):
    return v.reshape(S, R, v.shape[-1])


def fwd_kernel(x_hbm, w_hbm, b_ref, gates_hbm, cp_hbm, hp_hbm, xs_hbm, xl_hbm,
               w, xbuf, xout, gates, cprev, hprev, z0, z1, wsem, insem, recv, send, lastsem, osem):
    base, index, stage = place()
    first, last = stage == 0, stage == S - 1
    nxt = base + gray(lax.rem(stage + 1, S))
    plane_signal(base, index)
    wcopy = pltpu.make_async_copy(w_hbm.at[stage], w, wsem.at[0])
    wcopy.start()
    plane_wait()

    def feed(k):
        ts = pl.ds(k * CH, CH)

        @pl.when(first)
        def _():
            pltpu.make_async_copy(x_hbm.at[ts], xbuf.at[ts, 0], recv.at[k * CH]).start()

        @pl.when(jnp.logical_not(first))
        def _():
            pltpu.make_async_remote_copy(x_hbm.at[ts], xbuf.at[ts, index], insem, recv.at[k * CH],
                                         device_id=(base,), device_id_type=MESH).start()

        return 0

    def step_out(t):
        return pltpu.make_async_remote_copy(xout.at[t], xbuf.at[t], send, recv.at[t], device_id=(nxt,), device_id_type=MESH)

    def final_out(t, i):
        ts = pl.ds(t, CH)
        if i == LAST:
            return pltpu.make_async_copy(xout.at[ts, i], xl_hbm.at[ts], lastsem)
        return pltpu.make_async_remote_copy(xout.at[ts, i], xl_hbm.at[ts], send, lastsem, device_id=(base + i,), device_id_type=MESH)

    def arrived(t):
        @pl.when(jnp.logical_not(first))
        def _():
            step_out(t).wait_recv()

        @pl.when(first & (lax.rem(t, CH) == 0))
        def _():
            ts = pl.ds(t, CH)
            pltpu.make_async_remote_copy(xout.at[ts], xbuf.at[ts], send, recv.at[t], device_id=(nxt,), device_id_type=MESH).wait_recv()

    def pass_on(t):
        @pl.when(jnp.logical_not(last))
        def _():
            step_out(t).start()

        @pl.when(last & (lax.rem(t, CH) == CH - 1))
        def _():
            for i in range(S):
                final_out(t - CH + 1, i).start()

    lax.fori_loop(0, T // CH, lambda k, _: feed(k), 0)
    bias = b_ref[pl.ds(stage, 1), :]

    def project(zref, t):
        xt = rows_of(xbuf[t].astype(F32)).astype(BF16)
        for n in range(0, G4, HB):
            zref[:, n:n + HB] = dot(xt, w[0:H, n:n + HB]) + bias[:, n:n + HB]

    wcopy.wait()
    arrived(jnp.int32(0))
    project(z0, 0)

    kept = ((gates, gates_hbm), (cprev, cp_hbm), (hprev, hp_hbm), (xbuf, xs_hbm))

    def save(t):
        for i, (src, dst) in enumerate(kept):
            pltpu.make_async_copy(src.at[t], dst.at[t], osem.at[i]).start()

    def two(p, state):
        for u in range(2):
            t = 2 * p + u
            zc, zn = ((z0, z1), (z1, z0))[u]

            @pl.when(t > 0)
            def _():
                pass_on(t - 1)
                save(t - 1)

            @pl.when(t + 1 < T)
            def _():
                arrived(t + 1)

            ha, hc, ca, cc = state
            hlow = jnp.concatenate([ha, hc], axis=1).astype(BF16)
            hprev[t] = hlow
            cprev[t, :, 0:HB] = ca
            cprev[t, :, HB:H] = cc
            nh, nc = [], []
            for q in range(2):
                zz = []
                for g in range(4):
                    cols = slice(g * H + q * HB, g * H + q * HB + HB)
                    zz.append(zc[:, cols] + dot(hlow, w[H:2 * H, cols]))
                gi, gf, gg, go = jax.nn.sigmoid(zz[0]), jax.nn.sigmoid(zz[1]), jnp.tanh(zz[2]), jax.nn.sigmoid(zz[3])
                cn = gf * (ca, cc)[q] + gi * gg
                nh.append(go * jnp.tanh(cn))
                nc.append(cn)
                for g, val in enumerate((gi, gf, gg, go)):
                    gates[t, :, g * H + q * HB:g * H + q * HB + HB] = val
            project(zn, jnp.minimum(t + 1, T - 1))
            xt = rows_of(xbuf[t].astype(F32))
            xout[t] = groups_of(xt + jnp.concatenate(nh, axis=1)).astype(BF16)
            state = (nh[0], nh[1], nc[0], nc[1])
        return state

    zero = jnp.zeros((Q, HB), F32)
    lax.fori_loop(0, T // 2, two, (zero,) * 4)
    pass_on(jnp.int32(T - 1))
    save(T - 1)
    for i, (src, dst) in enumerate(kept):
        pltpu.make_async_copy(src, dst, osem.at[i]).wait()

    @pl.when(jnp.logical_not(first))
    def _():
        pltpu.make_async_remote_copy(x_hbm, xl_hbm, insem, lastsem, device_id=(base,), device_id_type=MESH).wait_send()

    @pl.when(jnp.logical_not(last))
    def _():
        pltpu.make_async_remote_copy(xout, xbuf, send, recv.at[0], device_id=(nxt,), device_id_type=MESH).wait_send()

    @pl.when(last)
    def _():
        others = (slice(None), slice(0, S - 1))
        pltpu.make_async_remote_copy(xout.at[others], xbuf.at[others], send, recv.at[0], device_id=(nxt,), device_id_type=MESH).wait_send()

    pltpu.make_async_copy(x_hbm, xl_hbm, lastsem).wait()


def forward(x, w, b):
    return pl.pallas_call(
        fwd_kernel,
        out_shape=(jax.ShapeDtypeStruct((T, Q, G4), F32), jax.ShapeDtypeStruct((T, Q, H), F32),
                   jax.ShapeDtypeStruct((T, Q, H), BF16), jax.ShapeDtypeStruct((T, S, R, H), BF16),
                   jax.ShapeDtypeStruct((T, R, H), BF16)),
        in_specs=[ANY, ANY, VMEM],
        out_specs=(HBM,) * 5,
        scratch_shapes=[pltpu.VMEM((2 * H, G4), BF16), pltpu.VMEM((T, S, R, H), BF16), pltpu.VMEM((T, S, R, H), BF16),
                        pltpu.VMEM((T, Q, G4), F32), pltpu.VMEM((T, Q, H), F32), pltpu.VMEM((T, Q, H), BF16)]
        + [pltpu.VMEM((Q, G4), F32)] * 2 + [DMA((1,)), DMA, DMA((T,)), DMA, DMA, DMA((4,))],
        compiler_params=pltpu.CompilerParams(vmem_limit_bytes=52 * MIB, collective_id=0, has_side_effects=True),
        cost_estimate=pl.CostEstimate(flops=60_000_000_000, bytes_accessed=80_000_000, transcendentals=0),
        name="lstm_fwd",
    )(x, w, b)


def bwd_kernel(d_hbm, gates_hbm, cp_hbm, hp_hbm, xs_hbm, w_hbm, both, own1, own2, give1, give2, db_ref, dx_hbm,
               w, wt, dbuf, dout, dall, ut, acc, gin, cin, hin, xin,
               wsem, insem, recv, send, lastsem, isem, osem):
    base, index, stage = place()
    plane = base // S
    first, last = stage == 0, stage == S - 1
    prv = base + gray(lax.rem(stage + S - 1, S))
    top = base + LAST
    plane_signal(base, index)
    wcopy = pltpu.make_async_copy(w_hbm.at[stage], w, wsem.at[0])
    wcopy.start()

    def feed(k):
        t = T - CH - k * CH
        ts = pl.ds(t, CH)

        @pl.when(last)
        def _():
            pltpu.make_async_copy(d_hbm.at[ts], dbuf.at[ts, LAST], recv.at[t]).start()

        @pl.when(jnp.logical_not(last))
        def _():
            pltpu.make_async_remote_copy(d_hbm.at[ts], dbuf.at[ts, index], insem, recv.at[t],
                                         device_id=(top,), device_id_type=MESH).start()

        return 0

    def step_out(t):
        return pltpu.make_async_remote_copy(dout.at[t], dbuf.at[t], send, recv.at[t], device_id=(prv,), device_id_type=MESH)

    def final_out(t, i):
        ts = pl.ds(t, CH)
        if i == 0:
            return pltpu.make_async_copy(dout.at[ts, i], dx_hbm.at[ts], lastsem)
        return pltpu.make_async_remote_copy(dout.at[ts, i], dx_hbm.at[ts], send, lastsem, device_id=(base + i,), device_id_type=MESH)

    def arrived(t):
        @pl.when(jnp.logical_not(last))
        def _():
            step_out(t).wait_recv()

        @pl.when(last & (lax.rem(t, CH) == CH - 1))
        def _():
            ts = pl.ds(t - CH + 1, CH)
            pltpu.make_async_remote_copy(dout.at[ts], dbuf.at[ts], send, recv.at[t - CH + 1], device_id=(prv,), device_id_type=MESH).wait_recv()

    def pass_on(t):
        @pl.when(jnp.logical_not(first))
        def _():
            step_out(t).start()

        @pl.when(first & (lax.rem(t, CH) == 0))
        def _():
            for i in range(S):
                final_out(t, i).start()

    def loads(t):
        k = lax.rem(t, NR)
        return [pltpu.make_async_copy(src.at[t], dst.at[k], isem.at[k, i])
                for i, (src, dst) in enumerate(((gates_hbm, gin), (cp_hbm, cin), (hp_hbm, hin), (xs_hbm, xin)))]

    for t in range(T - NR, T):
        for cp in loads(t):
            cp.start()
    plane_wait()
    lax.fori_loop(0, T // CH, lambda k, _: feed(k), 0)
    db_ref[...] = jnp.zeros(db_ref.shape, F32)
    acc[...] = jnp.zeros(acc.shape, F32)
    wcopy.wait()

    def turn(n, _):
        cols = pl.ds(pl.multiple_of(n * HB, HB), HB)
        wt[cols, :] = w[:, cols].T
        return 0

    lax.fori_loop(0, G4 // HB, turn, 0)

    def weight():
        def part(k, _):
            for n in range(0, 2 * H, HB):
                cols = pl.ds(pl.multiple_of(k * 2 * H + n, HB), HB)
                acc[:, cols] += dot(ut[...], dall[:, cols])
            return 0

        lax.fori_loop(0, G4 // (2 * H), part, 0)

    def two(n, state):
        p = T // 2 - 1 - n
        us = []
        for u in (1, 0):
            t = 2 * p + u
            k = lax.rem(t, NR)
            for cp in loads(t):
                cp.wait()

            @pl.when(t < T - 1)
            def _():
                pass_on(t + 1)

            if u == 1:
                @pl.when((p < T // 2 - 1) & (lax.rem(p, CH // 2) == CH // 2 - 1))
                def _():
                    weight()

            arrived(t)
            ea, ec, da, dc_ = state
            dext = rows_of(dbuf[t])
            parts = [[None, None] for _ in range(4)]
            nd = []
            for q in range(2):
                gi, gf, gg, go = (gin[k, :, g * H + q * HB:g * H + q * HB + HB] for g in range(4))
                hq = slice(q * HB, q * HB + HB)
                cprev = cin[k, :, hq]
                th = jnp.tanh(gf * cprev + gi * gg)
                e = dext[:, hq] + (ea, ec)[q]
                dc = (da, dc_)[q] + e * (go * (1.0 - th * th))
                parts[0][q] = dc * (gg * gi * (1.0 - gi))
                parts[1][q] = dc * (cprev * gf * (1.0 - gf))
                parts[2][q] = dc * (gi * (1.0 - gg * gg))
                parts[3][q] = e * (th * go * (1.0 - go))
                nd.append(dc * gf)
            trows = pl.ds(pl.multiple_of(lax.rem(t, CH) * Q, Q), Q)
            lows = []
            for i, v in enumerate(v for ps in parts for v in ps):
                cols = slice(i * HB, i * HB + HB)
                low = v.astype(BF16)
                dall[trows, cols] = low
                lows.append(low)
                db_ref[:, cols] += jnp.sum(v.reshape(Q // R, R, HB), axis=0)
            lowz = jnp.concatenate(lows, axis=1)
            ne = [dot(lowz, wt[:, H + q * HB:H + q * HB + HB]) for q in range(2)]
            for q in range(2):
                hq = slice(q * HB, q * HB + HB)
                dout[t, :, :, hq] = groups_of(dext[:, hq] + dot(lowz, wt[:, hq]))
            state = (ne[0], ne[1], nd[0], nd[1])
            us.append((rows_of(xin[k].astype(F32)), hin[k].astype(F32)))

            @pl.when(t >= NR)
            def _():
                for cp in loads(t - NR):
                    cp.start()

        tcols = pl.ds(pl.multiple_of(lax.rem(p, CH // 2) * 2 * Q, 2 * Q), 2 * Q)
        for j in range(2):
            ut[j * H:j * H + H, tcols] = jnp.concatenate([us[1][j], us[0][j]], axis=0).T.astype(BF16)

        return state

    zero = jnp.zeros((Q, HB), F32)
    lax.fori_loop(0, T // 2, two, (zero,) * 4)
    pass_on(jnp.int32(0))

    weight()
    outs = []
    for i, (dst, (row, step, rows), at) in enumerate(((both, PIECES[0], 0), (give1, PIECES[1], 1 - plane), (give2, PIECES[2], 1 - plane),
                                                      (own1, PIECES[1], plane), (own2, PIECES[2], plane))):
        outs.append(pltpu.make_async_copy(acc.at[pl.ds(pl.multiple_of(row + at * step, LANE), rows)], dst, osem.at[i]))
        outs[i].start()
    for out in outs:
        out.wait()

    @pl.when(jnp.logical_not(last))
    def _():
        pltpu.make_async_remote_copy(d_hbm, dx_hbm, insem, lastsem, device_id=(top,), device_id_type=MESH).wait_send()

    @pl.when(jnp.logical_not(first))
    def _():
        pltpu.make_async_remote_copy(dout, dbuf, send, recv.at[0], device_id=(prv,), device_id_type=MESH).wait_send()

    @pl.when(first)
    def _():
        others = (slice(None), slice(1, S))
        pltpu.make_async_remote_copy(dout.at[others], dbuf.at[others], send, recv.at[0], device_id=(prv,), device_id_type=MESH).wait_send()

    pltpu.make_async_copy(d_hbm, dx_hbm, lastsem).wait()


def backward(d_top, gates, cprev, hprev, xs, w):
    return pl.pallas_call(
        bwd_kernel,
        out_shape=tuple(jax.ShapeDtypeStruct((rows, G4), F32) for _, _, rows in PIECES + PIECES[1:]) + (jax.ShapeDtypeStruct((R, G4), F32), jax.ShapeDtypeStruct((T, R, H), F32)),
        in_specs=[ANY] * 6,
        out_specs=(HBM,) * 5 + (VMEM, HBM),
        scratch_shapes=[pltpu.VMEM((2 * H, G4), BF16), pltpu.VMEM((G4, 2 * H), BF16), pltpu.VMEM((T, S, R, H), F32),
                        pltpu.VMEM((T, S, R, H), F32), pltpu.VMEM((CH * Q, G4), BF16), pltpu.VMEM((2 * H, CH * Q), BF16), pltpu.VMEM((2 * H, G4), F32)]
        + [pltpu.VMEM((NR, Q, G4), F32), pltpu.VMEM((NR, Q, H), F32), pltpu.VMEM((NR, Q, H), BF16), pltpu.VMEM((NR, S, R, H), BF16)]
        + [DMA((1,)), DMA, DMA((T,)), DMA, DMA, DMA((NR, 4)), DMA((5,))],
        compiler_params=pltpu.CompilerParams(vmem_limit_bytes=56 * MIB, collective_id=1, has_side_effects=True),
        cost_estimate=pl.CostEstimate(flops=110_000_000_000, bytes_accessed=80_000_000, transcendentals=0),
        name="lstm_bwd",
    )(d_top, gates, cprev, hprev, xs, w)


VB = 1280
NVB = V // VB
N = T * R
NW = 4
RB = 64


def head_kernel(x_ref, t_ref, w_hbm, dx_ref, lse_ref, lg, g0, g1, wv, mx, sm, tb, wsem):
    def wcopy(b):
        buf = lax.rem(b, NW)
        return pltpu.make_async_copy(w_hbm.at[:, pl.ds(pl.multiple_of(lax.rem(b, NVB) * VB, VB), VB)], wv.at[buf], wsem.at[buf])

    for b in range(NW - 1):
        wcopy(b).start()

    def ready(b):
        for i in range(2):
            wcopy(b + i).wait()
            wcopy(b + i + 2).start()

    mx[...] = jnp.full(mx.shape, -jnp.inf, F32)
    sm[...] = jnp.zeros(sm.shape, F32)
    dx_ref[...] = jnp.zeros(dx_ref.shape, F32)

    def each(n, act):
        lax.fori_loop(0, n, lambda i, _: (act(i), 0)[1], 0)

    def at(i, size):
        return pl.ds(pl.multiple_of(i * size, size), size)

    def logits(b, cols):
        lg[b, :, cols] = dot(x_ref[...], wv[lax.rem(b, NW), :, cols])

    def sums(b, rows):
        m_old = mx[rows, :]
        m_new = m_old
        for c in range(0, VB, LANE):
            m_new = jnp.maximum(m_new, lg[b, rows, c:c + LANE])
        acc = sm[rows, :] * jnp.exp(m_old - m_new)
        for c in range(0, VB, LANE):
            acc = acc + jnp.exp(lg[b, rows, c:c + LANE] - m_new)
        mx[rows, :] = m_new
        sm[rows, :] = acc

    wcopy(0).wait()
    each(VB // HB, lambda c: logits(0, at(c, HB)))

    def first(h, _):
        b = 2 * h + 1
        ready(b)
        for i in range(2):
            for c in range(0, VB, HB):
                logits(b + i, slice(c, c + HB))
            for r in range(0, N, RB):
                sums(b + i - 1, slice(r, r + RB))
        return 0

    lax.fori_loop(0, NVB // 2, first, 0)
    each(N // RB, lambda r: sums(NVB - 1, at(r, RB)))

    def finish(r):
        rows = at(r, LANE)
        top = jnp.max(mx[rows, :], axis=1, keepdims=True)
        tot = jnp.sum(sm[rows, :] * jnp.exp(mx[rows, :] - top), axis=1, keepdims=True)
        lse = top + jnp.log(tot)
        lse_ref[rows, :] = lse
        mx[rows, :] = jnp.broadcast_to(lse, (LANE, LANE))
        tb[rows, :] = jnp.broadcast_to(t_ref[rows, :], (LANE, LANE))

    each(N // LANE, finish)

    def grads(b, gb, c):
        ids = [b * VB + c + h + lax.broadcasted_iota(jnp.int32, (RB, LANE), 1) for h in (0, LANE)]
        for r in range(0, N, RB):
            rows = slice(r, r + RB)
            lse = mx[rows, :]
            for h in (0, LANE):
                cols = pl.ds(c + h, LANE)
                p = jnp.exp(lg[b, rows, cols] - lse)
                gb[rows, cols] = jnp.where(tb[rows, :] == ids[h // LANE], p - 1.0, p).astype(BF16)

    def apply(b, gb, cols):
        return dot_tt(gb[:, cols], wv[lax.rem(b + NVB, NW), :, cols])

    each(VB // HB, lambda c: grads(0, g0, pl.multiple_of(c * HB, HB)))

    def second(h, _):
        for i in range(2):
            b = 2 * h + NVB + i
            wcopy(b).wait()

            @pl.when(b + 2 < 2 * NVB)
            def _():
                wcopy(b + 2).start()

        for b, gb, gn in ((2 * h, g0, g1), (2 * h + 1, g1, g0)):
            total = jnp.zeros((N, H), F32)
            for c in range(0, VB, HB):
                total = total + apply(b, gb, slice(c, c + HB))
                grads(b + 1, gn, c)
            dx_ref[...] += total
        return 0

    lax.fori_loop(0, NVB // 2, second, 0)
    wcopy(2 * NVB - 1).wait()

    def last(c):
        dx_ref[...] += apply(NVB - 1, g0, at(c, HB))

    each(VB // HB, last)


def head(x, tgt, w_vocab):
    return pl.pallas_call(
        head_kernel,
        out_shape=(jax.ShapeDtypeStruct((N, H), F32), jax.ShapeDtypeStruct((N, 1), F32)),
        in_specs=[VMEM, VMEM, ANY],
        out_specs=(VMEM, VMEM),
        scratch_shapes=[pltpu.VMEM((NVB, N, VB), F32), pltpu.VMEM((N, VB), BF16), pltpu.VMEM((N, VB), BF16), pltpu.VMEM((NW, H, VB), BF16),
                        pltpu.VMEM((N, LANE), F32), pltpu.VMEM((N, LANE), F32), pltpu.VMEM((N, LANE), jnp.int32), DMA((NW,))],
        compiler_params=pltpu.CompilerParams(vmem_limit_bytes=60 * MIB),
        cost_estimate=pl.CostEstimate(flops=40_000_000_000, bytes_accessed=70_000_000, transcendentals=0),
        name="head",
    )(x, tgt, w_vocab)


TB = 768
NTOK = NDEV * N
NK = NTOK // TB
UN = 2
NOWN = (NVB + 1) // 2


def dwv_kernel(lo, hi, came, x_hbm, st_ref, w_hbm, *rest):
    nshared = min(hi, NOWN - 1) - lo
    arrived = rest[len(rest) - 15 - 1 - (nshared > 0) - len(came):]
    dw_hbm = arrived[len(came)]
    give_hbm = arrived[len(came) + 1]
    xv, xtv, wv, g0, g1, acc, lse, tgt, box, wsem, xsem, osem, gsem, isem, psem = rest[-15:]
    core = lax.rem(lax.axis_index("data"), 2)

    def block(j, side):
        return j + side * (NVB - 1 - 2 * j)

    def cols(b):
        return pl.ds(pl.multiple_of(b * VB, VB), VB)

    def wcopy(i):
        buf = lax.rem(i, 2)
        return pltpu.make_async_copy(w_hbm.at[:, cols(block(lo + i, core))], wv.at[buf], wsem.at[buf])

    def keep(i):
        buf = lax.rem(i, 2)
        return pltpu.make_async_copy(acc.at[buf], dw_hbm.at[:, cols(block(lo + i, core))], osem.at[buf])

    def give(i):
        buf = lax.rem(i, 2)
        return pltpu.make_async_copy(acc.at[buf], give_hbm.at[i], gsem.at[buf])

    def done(i):
        keep(i).start()
        if nshared > 0:
            give(i).start()

    def drained(i):
        keep(i).wait()
        if nshared > 0:
            give(i).wait()

    pieces = [(src, first, i, r) for src, (first, count) in zip(arrived, came) for i in range(count) for r in range(0, H, LANE)]
    per = -(-len(pieces) // ((hi - lo) * NK // UN))

    def fetch(src, i, r, k, slot):
        return pltpu.make_async_copy(src.at[i, pl.ds(r, LANE)], box.at[k, slot], isem.at[k, slot])

    def put(first, i, r, k, slot):
        return pltpu.make_async_copy(box.at[k, slot], dw_hbm.at[pl.ds(r, LANE), cols(block(first + i, 1 - core))], psem.at[k, slot])

    def pieces_of(h, act):
        at = 0
        for src, (first, count) in zip(arrived, came):
            total = count * H // LANE
            for slot in range(per):
                c = h * per + slot - at
                i, r = c // (H // LANE), pl.multiple_of(lax.rem(c, H // LANE) * LANE, LANE)

                @pl.when((c >= 0) & (c < total))
                def _():
                    act(src, first, i, r, lax.rem(h, 2), slot)

            at += total

    def land(src, first, i, r, k, slot):
        fetch(src, i, r, k, slot).wait()
        put(first, i, r, k, slot).start()

    def move(h):
        if came:
            pieces_of(h, land)
            pieces_of(h - 1 + 2 * (h == 0) * len(pieces), lambda src, first, i, r, k, slot: put(first, i, r, k, slot).wait())
            pieces_of(h + 1, lambda src, first, i, r, k, slot: fetch(src, i, r, k, slot).start())

    n = hi - lo
    wcopy(0).start()
    cx = pltpu.make_async_copy(x_hbm, xv, xsem.at[0])
    cx.start()
    cx.wait()

    def turn(k, _):
        for c in range(0, TB, HB):
            rows = pl.ds(pl.multiple_of(k * TB + c, HB), HB)
            xtv[k, :, c:c + HB] = xv[rows, :].T
            lse[rows, :] = jnp.broadcast_to(st_ref[rows, 0:1], (HB, LANE))
            tgt[rows, :] = jnp.broadcast_to(st_ref[rows, LANE - 1:LANE], (HB, LANE))
        return 0

    lax.fori_loop(0, NK, turn, 0)
    if came:
        pieces_of(jnp.int32(0), lambda src, first, i, r, k, slot: fetch(src, i, r, k, slot).start())

    def weight(it, gold, cols, reset=False):
        k, i = lax.rem(it + NK, NK), jnp.maximum(it, 0) // NK
        acc_c = acc.at[lax.rem(i, 2), :, cols]
        old = acc_c[...]
        acc_c[...] = (jnp.where(k == 0, 0.0, old) if reset else old) + dot(xtv[k], gold[:, cols])

    def step(it, u):
        gnew, gold = ((g0, g1), (g1, g0))[u % 2]
        k, i = lax.rem(it, NK) + u, it // NK
        base = pl.multiple_of(k * TB, TB)
        lane = lax.broadcasted_iota(jnp.int32, (R, LANE), 1) + block(lo + i, core) * VB
        for c in range(0, VB, HB):
            lgt = dot(xv[pl.ds(base, TB), :], wv[lax.rem(i, 2), :, c:c + HB])
            weight(it + u - 1, gold, slice(c, c + HB), u == 1)
            ids = [jnp.tile((lane + (c + h)).astype(F32), (RB // R, 1)) for h in (0, LANE)]
            for r in range(0, TB, RB):
                here = pl.ds(pl.multiple_of(base + r, RB), RB)
                for h in (0, LANE):
                    p = jnp.exp(lgt[r:r + RB, h:h + LANE] - lse[here, :])
                    gnew[r:r + RB, c + h:c + h + LANE] = jnp.where(tgt[here, :] == ids[h // LANE], p - 1.0, p).astype(BF16)

    def body(h, _):
        it = UN * h
        i0, k0 = it // NK, lax.rem(it, NK)
        move(h)

        @pl.when(k0 == 0)
        def _():
            wcopy(i0).wait()

            @pl.when(i0 < n - 1)
            def _():
                wcopy(i0 + 1).start()

        @pl.when((k0 == 0) & (i0 >= 2))
        def _():
            drained(i0 - 2)

        for u in range(UN):
            step(it, u)

        @pl.when((k0 == UN) & (i0 >= 1))
        def _():
            done(i0 - 1)

        return 0

    lax.fori_loop(0, n * NK // UN, body, 0)

    def last(c, _):
        weight(jnp.int32(n * NK - 1), g1, pl.ds(pl.multiple_of(c * HB, HB), HB))
        return 0

    lax.fori_loop(0, VB // HB, last, 0)
    if n > 1:
        drained(n - 2)
    done(n - 1)
    if came:
        pieces_of(jnp.int32(n * NK // UN - 1), lambda src, first, i, r, k, slot: put(first, i, r, k, slot).wait())
    drained(n - 1)


def grad_vocab(lo, hi, x_all, stats, w_vocab, before=(), came=()):
    counts = tuple((first, v.shape[0]) for first, v in came)
    nshared = min(hi, NOWN - 1) - lo
    out = (jax.ShapeDtypeStruct((H, V), F32), jax.ShapeDtypeStruct((nshared, H, VB), F32))[:1 + (nshared > 0)]
    per = max(1, -(-sum(c for _, c in counts) * (H // LANE) // ((hi - lo) * NK // UN)))
    return pl.pallas_call(
        functools.partial(dwv_kernel, lo, hi, counts),
        out_shape=out,
        in_specs=[ANY, VMEM, ANY] + [HBM] * (len(before) + len(came)),
        out_specs=(HBM,) * len(out),
        input_output_aliases={3: 0} if before else {},
        scratch_shapes=[pltpu.VMEM((NTOK, H), BF16), pltpu.VMEM((NK, H, TB), BF16), pltpu.VMEM((2, H, VB), BF16)]
        + [pltpu.VMEM((TB, VB), BF16)] * 2
        + [pltpu.VMEM((2, H, VB), F32)] + [pltpu.VMEM((NTOK, LANE), F32)] * 2 + [pltpu.VMEM((2, per, LANE, VB), F32)]
        + [DMA((2,)), DMA((1,)), DMA((2,)), DMA((2,)), DMA((2, per)), DMA((2, per))],
        compiler_params=pltpu.CompilerParams(vmem_limit_bytes=62 * MIB),
        cost_estimate=pl.CostEstimate(flops=(hi - lo) * 20_000_000_000, bytes_accessed=100_000_000, transcendentals=0),
        name="dwv",
    )(x_all, stats, w_vocab, *before, *(v for _, v in came))


NC = 8


def copy_ring(n, src, dst, buf, isem, osem):
    def fetch(i):
        k = lax.rem(i, NC)
        return pltpu.make_async_copy(src(i), buf.at[k], isem.at[k])

    def put(i):
        k = lax.rem(i, NC)
        return pltpu.make_async_copy(buf.at[k], dst(i), osem.at[k])

    for i in range(NC // 2):
        fetch(i).start()

    def body(i, _):
        fetch(i).wait()
        put(i).start()

        @pl.when(i >= NC // 2)
        def _():
            put(i - NC // 2).wait()

        @pl.when(i + NC // 2 < n)
        def _():
            fetch(i + NC // 2).start()

        return 0

    lax.fori_loop(0, n, body, 0)
    for i in range(n - NC // 2, n):
        put(i).wait()


def copy_call(kernel, out, block, args):
    return pl.pallas_call(
        kernel,
        out_shape=jax.ShapeDtypeStruct(out, F32),
        in_specs=[HBM] * len(args),
        out_specs=HBM,
        input_output_aliases={1: 0} if len(args) > 1 else {},
        scratch_shapes=[pltpu.VMEM((NC,) + block, F32), DMA((NC,)), DMA((NC,))],
        compiler_params=pltpu.CompilerParams(vmem_limit_bytes=24 * MIB),
        cost_estimate=pl.CostEstimate(flops=20_000_000_000, bytes_accessed=130_000_000, transcendentals=0),
    )(*args)


def place_dw(piece, parts, *before):
    row, step, rows = PIECES[piece]

    def kernel(src, *rest):
        dst, scratch = rest[-4], rest[-3:]

        def target(i):
            return dst.at[gray(lax.rem(i, S)), pl.ds(pl.multiple_of(row + i // S * step, LANE), rows)]

        copy_ring(parts.shape[0], lambda i: src.at[i, 0:rows], target, *scratch)

    return copy_call(kernel, (L, 2 * H, G4), (rows, G4), (parts,) + before)


SPLITS = (0, 2, 5, 12, NOWN)


def solution(mesh):
    def local_grads(x_rows, tgt_rows, w_lstm, b_lstm, w_vocab):
        tgt = jnp.swapaxes(tgt_rows, 0, 1).reshape(N, 1)
        gates, cprev, hprev, xs, top = forward(jnp.swapaxes(x_rows, 0, 1), w_lstm, b_lstm)
        top = top.reshape(N, H)
        d_top, lse = head(top, tgt, w_vocab)
        half = (N, LANE // 2)
        stats = jnp.concatenate([jnp.broadcast_to(lse, half), jnp.broadcast_to(tgt.astype(F32), half)], axis=1)
        x_all = lax.all_gather(top, 'data', axis=0, tiled=True)
        stats = lax.all_gather(stats, 'data', axis=0, tiled=True)
        d_top, x_all = lax.optimization_barrier((d_top, x_all))
        both, *owns, give1, give2, db, dx = backward(d_top.reshape(T, R, H), gates, cprev, hprev, xs, w_lstm)
        other_plane = [(i, (i + S) % NDEV) for i in range(NDEV)]
        other_core = [(i, i + 1 - 2 * (i % 2)) for i in range(NDEV)]
        planes = [list(range(S)), list(range(S, NDEV))]
        dwv, part, gathered, swapped = (), both, [], []
        for i, (own, give) in enumerate(((both, both), (owns[0], give1), (owns[1], give2))):
            if i:
                give, part = lax.optimization_barrier((give, part))
            got = lax.ppermute(give, 'data', other_plane)
            dwv, sent = grad_vocab(SPLITS[i], SPLITS[i + 1], x_all, stats, w_vocab, dwv, swapped[:1] if i == 2 else ())
            own, dwv = lax.optimization_barrier((own, dwv))
            part = own + got if i != 1 else jnp.concatenate([own + got, db], axis=0)
            part, dwv = lax.optimization_barrier((part, dwv))
            gathered.append(lax.all_gather(part, 'data', axis=0, axis_index_groups=None if i else planes))
            swapped.append((SPLITS[i], lax.ppermute(sent, 'data', other_core)))
            dwv = (dwv,)
        dwv, = grad_vocab(SPLITS[3], SPLITS[4], x_all, stats, w_vocab, dwv, swapped[1:])
        dw = place_dw(0, gathered[0])
        dw = place_dw(2, gathered[2], place_dw(1, gathered[1], dw))
        db = gathered[1][:, PIECES[1][2]:].reshape(NDEV // S, S, R, G4).sum(axis=(0, 2))
        db = jnp.stack([db[gray(i)] for i in range(L)])
        return dw, db, dwv, jnp.swapaxes(dx, 0, 1)

    return jax.shard_map(local_grads, mesh=mesh, in_specs=(P('data'), P('data'), P(), P(), P()), out_specs=(P(), P(), P(), P('data')), check_vma=False)
```

profile of v0, /device:TPU:0, one launch (start us, length us, event | category | flops | bytes accessed | tf_op | source)
XLA Modules:
  0.0 679.3 jit_solution(5018696357099244729)
XLA Ops:
  7.2 0.0 all-gather.9.cloned.1.call-start
  7.2 1.2 copy.28
  8.4 0.8 copy-done.2
  9.3 83.5 %lstm_fwd.1 = (f32[48,64,2048]{2,1,0:T(8,128)}, f32[48,64,512]{2,1,0:T(8,128)}, bf16[48,64,512]{2,1,0:T(8,128)(2,1)}, bf16[48,8,8,512]{3,2,1,0:T(8,128)(2,1)}, bf16[48,8,512]{2,1,0:T(8,128)(2,1)}) custom-call(bf16[48,8,512]{2,1,0:T(8,128)(2,1)S(1)} %bitcast.15, bf16[8,1024,2048]{2,1,0:T(8,128)(2,1)} %w_hbm.9, f32[8,2048]{1,0:T(8,128)S(1)} %copy-done.2), custom_call_target="tpu_custom_call" | custom-call | flops 60000002048 | bytes 80000000 | tf_op jit(solution)/shard_map/lstm_fwd/pallas_call | solution.py:207
  92.7 0.0 all-gather.9.cloned.1.call-update
  92.8 0.0 all-gather.11.cloned.1.call-start
  92.8 0.1 copy.23
  92.9 0.8 reshape.33.t_ref
  93.7 0.1 copy.25
  93.8 0.1 convert_element_type.12
  93.9 46.0 %head.1 = (f32[384,512]{1,0:T(8,128)}, f32[384,1]{1,0:T(8,128)}) custom-call(bf16[384,512]{1,0:T(8,128)(2,1)} %bitcast.1.x_ref, s32[384,1]{1,0:T(8,128)} %reshape.33.t_ref, bf16[512,32000]{1,0:T(8,128)(2,1)} %w_hbm.13), custom_call_target="tpu_custom_call" | custom-call | flops 40000000000 | bytes 70000000 | tf_op jit(solution)/shard_map/head/pallas_call | solution.py:529
  139.9 1.1 reduce.2
  141.0 0.1 broadcast_in_dim.13
  141.1 0.1 broadcast_in_dim.14
  141.2 0.8 pad_maximum_fusion.1
  142.0 0.0 all-gather.11.cloned.1.call-update
  142.0 0.0 all-gather.17.cloned.1.call-start
  142.1 0.0 all-gather.9.cloned.1.call-done.x_hbm
  142.1 132.1 %lstm_bwd.1 = (f32[256,2048]{1,0:T(8,128)}, f32[256,2048]{1,0:T(8,128)}, f32[128,2048]{1,0:T(8,128)}, f32[256,2048]{1,0:T(8,128)}, f32[128,2048]{1,0:T(8,128)}, ...) custom-call(f32[48,8,512]{2,1,0:T(8,128)} %bitcast.20, f32[48,64,2048]{2,1,0:T(8,128)} %get-tuple-element.43.gates_hbm, ...), custom_call_target="tpu_custom_call" | custom-call | flops 109999996928 | bytes 80000000 | tf_op jit(solution)/shard_map/lstm_bwd/pallas_call | solution.py:401
  274.2 1.5 collective-permute-start
  275.7 47.2 %dwv.4 = (f32[512,32000]{1,0:T(8,128)}, f32[2,512,1280]{2,1,0:T(8,128)}) custom-call(bf16[6144,512]{1,0:T(8,128)(2,1)} %all-gather.9.cloned.1.call-done.x_hbm, f32[6144,128]{1,0:T(8,128)} %all-gather.11.cloned.1.call-done.st_ref, bf16[512,32000]{1,0:T(8,128)(2,1)} %w_hbm.13), custom_call_target="tpu_custom_call" | custom-call | flops 40000000000 | bytes 100000000 | tf_op jit(solution)/shard_map/dwv/pallas_call | solution.py:703
  322.9 3.9 add.9
  326.8 0.0 all-gather.15.cloned.1.call-start
  326.9 0.6 collective-permute-start.1
  327.5 65.3 %dwv.5 = (f32[512,32000]{1,0:T(8,128)}, f32[3,512,1280]{2,1,0:T(8,128)}) custom-call(bf16[6144,512]{1,0:T(8,128)(2,1)} %all-gather.9.cloned.1.call-done.x_hbm, f32[6144,128]{1,0:T(8,128)} %all-gather.11.cloned.1.call-done.st_ref, bf16[512,32000]{1,0:T(8,128)(2,1)} %w_hbm.13, f32[512,32000]{1,0:T(8,128)} %get-tuple-element.55.rest_0_), custom_call_target="tpu_custom_call", output_to_operand_aliasing={{0}: (3, {})} | custom-call | flops 60000002048 | bytes 100000000 | tf_op jit(solution)/shard_map/dwv/pallas_call | solution.py:703
  392.9 2.6 add.10
  395.5 1.5 pad_maximum_fusion
  397.0 0.3 all-gather.13.cloned.1.call-start
  397.3 0.0 collective-permute-start.2
  397.4 1.1 collective-permute-start.3
  398.5 9.3 %collective-permute-done.2.rest_1_ = f32[2,512,1280]{2,1,0:T(8,128)} collective-permute-done((f32[2,512,1280]{2,1,0:T(8,128)}, f32[2,512,1280]{2,1,0:T(8,128)}, u32[]{:S(2)}, u32[]{:S(2)}) %collective-permute-start.2) | collective-permute-done | bytes 5242912 | tf_op jit(solution)/shard_map/ppermute | solution.py:808
  407.8 134.7 %dwv.6 = (f32[512,32000]{1,0:T(8,128)}, f32[7,512,1280]{2,1,0:T(8,128)}) custom-call(bf16[6144,512]{1,0:T(8,128)(2,1)} %all-gather.9.cloned.1.call-done.x_hbm, f32[6144,128]{1,0:T(8,128)} %all-gather.11.cloned.1.call-done.st_ref, bf16[512,32000]{1,0:T(8,128)(2,1)} %w_hbm.13, ...), custom_call_target="tpu_custom_call", output_to_operand_aliasing={{0}: (3, {})} | custom-call | flops 140000002048 | bytes 100000000 | tf_op jit(solution)/shard_map/dwv/pallas_call | solution.py:703
  542.6 2.3 add.11
  544.9 0.1 collective-permute-start.5
  545.0 0.5 collective-permute-start.4
  545.5 1.3 copy.26
  546.8 39.4 %collective-permute-done.4.rest_1_ = f32[3,512,1280]{2,1,0:T(8,128)} collective-permute-done((f32[3,512,1280]{2,1,0:T(8,128)}, f32[3,512,1280]{2,1,0:T(8,128)}, u32[]{:S(2)}, u32[]{:S(2)}) %collective-permute-start.4) | collective-permute-done | bytes 7864352 | tf_op jit(solution)/shard_map/ppermute | solution.py:808
  586.2 37.5 %dwv.7 = f32[512,32000]{1,0:T(8,128)} custom-call(bf16[6144,512]{1,0:T(8,128)(2,1)} %all-gather.9.cloned.1.call-done.x_hbm, f32[6144,128]{1,0:T(8,128)} %all-gather.11.cloned.1.call-done.st_ref, bf16[512,32000]{1,0:T(8,128)(2,1)} %w_hbm.13, f32[512,32000]{1,0:T(8,128)} %get-tuple-element.72.rest_0_, ...), custom_call_target="tpu_custom_call", output_to_operand_aliasing={{}: (3, {})} | custom-call | flops 20000000000 | bytes 100000000 | tf_op jit(solution)/shard_map/dwv/pallas_call | solution.py:703
  623.7 0.0 all-gather.17.cloned.1.call-done
  623.7 6.1 copy-done
  629.8 6.6 shard_map.84.rest_0_
  636.4 0.0 all-gather.15.cloned.1.call-done
  636.5 1.5 slice_reduce_fusion
  638.0 22.1 %shard_map.85.rest_0_ = f32[8,1024,2048]{2,1,0:T(8,128)} custom-call(f32[16,264,2048]{2,1,0:T(8,128)} %bitcast.17, f32[8,1024,2048]{2,1,0:T(8,128)} %shard_map.84.rest_0_), custom_call_target="tpu_custom_call", output_to_operand_aliasing={{}: (1, {})} | custom-call | flops 20000000000 | bytes 130000000 | tf_op jit(solution)/shard_map/pallas_call | solution.py:754
  660.1 0.0 all-gather.13.cloned.1.call-done
  660.1 5.8 copy-done.1
  665.9 6.3 shard_map.86
  672.1 0.7 pad_maximum_fusion.2
  (26 shorter events, 0.1 us)
Async XLA Ops:
  7.2 134.9 %all-gather.9.cloned.1.call-start = ((), (), s32[]{:S(2)}) async-start(), calls=%async_computation | async-start | bytes 6684672 | tf_op jit(solution)/shard_map/all_gather | solution.py:791
  8.4 0.8 copy-start.2
  9.3 83.5 %copy-start.7 = (s32[8,48]{1,0:T(8,128)S(1)}, s32[8,48]{1,0:T(8,128)}, u32[]{:S(2)}) copy-start(s32[8,48]{1,0:T(8,128)} %param.6) | copy-start | bytes 4612
  92.8 183.0 %all-gather.11.cloned.1.call-start = ((), (), s32[]{:S(2)}) async-start(), calls=%async_computation.1 | async-start | bytes 3342336 | tf_op jit(solution)/shard_map/all_gather | solution.py:792
  142.0 481.7 %all-gather.17.cloned.1.call-start = ((), (), s32[]{:S(2)}) async-start(), calls=%async_computation.4 | async-start | bytes 18874368 | tf_op jit(solution)/shard_map/all_gather | solution.py:807
  274.2 48.7 %collective-permute-start = (f32[256,2048]{1,0:T(8,128)}, f32[256,2048]{1,0:T(8,128)}, u32[]{:S(2)}, u32[]{:S(2)}) collective-permute-start(f32[256,2048]{1,0:T(8,128)} %get-tuple-element.53), channel_id=1, source_target_pairs={{0,8},{1,9},{2,10},{3,11},{4,12},{5,13},{6,14},{7,15},{8,0},{9,1},... | collective-permute-start | bytes 6291464 | tf_op jit(solution)/shard_map/ppermute | solution.py:802
  326.8 309.6 %all-gather.15.cloned.1.call-start = ((), (), s32[]{:S(2)}) async-start(), calls=%async_computation.3 | async-start | bytes 36765696 | tf_op jit(solution)/shard_map/all_gather | solution.py:807
  326.9 66.0 %collective-permute-start.1 = (f32[256,2048]{1,0:T(8,128)}, f32[256,2048]{1,0:T(8,128)}, u32[]{:S(2)}, u32[]{:S(2)}) collective-permute-start(f32[256,2048]{1,0:T(8,128)} %get-tuple-element.60), channel_id=1, source_target_pairs={{0,8},{1,9},{2,10},{3,11},{4,12},{5,13},{6,14},{7,15},{8,0},{9,1},... | collective-permute-start | bytes 6291464 | tf_op jit(solution)/shard_map/ppermute | solution.py:802
  392.8 2.6 copy-start.6
  397.0 263.1 %all-gather.13.cloned.1.call-start = ((), (), s32[]{:S(2)}) async-start(), calls=%async_computation.2 | async-start | bytes 17825792 | tf_op jit(solution)/shard_map/all_gather | solution.py:807
  397.3 10.5 %collective-permute-start.2 = (f32[2,512,1280]{2,1,0:T(8,128)}, f32[2,512,1280]{2,1,0:T(8,128)}, u32[]{:S(2)}, u32[]{:S(2)}) collective-permute-start(f32[2,512,1280]{2,1,0:T(8,128)} %get-tuple-element.64), channel_id=1, source_target_pairs={{0,1},{1,0},{2,3},{3,2},{4,5},{5,4},{6,7},{7,6},{8,9},{9,8},{10,11... | collective-permute-start | bytes 15728648 | tf_op jit(solution)/shard_map/ppermute | solution.py:808
  397.3 145.2 %copy-start.3 = (f32[128,2048]{1,0:T(8,128)S(1)}, f32[128,2048]{1,0:T(8,128)}, u32[]{:S(2)}) copy-start(f32[128,2048]{1,0:T(8,128)} %get-tuple-element.66) | copy-start | bytes 3145732
  397.4 148.1 %copy-start.4 = (f32[48,8,512]{2,1,0:T(8,128)S(1)}, f32[48,8,512]{2,1,0:T(8,128)}, u32[]{:S(2)}) copy-start(f32[48,8,512]{2,1,0:T(8,128)} %get-tuple-element.75) | copy-start | bytes 2359300
  397.4 145.2 %collective-permute-start.3 = (f32[128,2048]{1,0:T(8,128)}, f32[128,2048]{1,0:T(8,128)}, u32[]{:S(2)}, u32[]{:S(2)}) collective-permute-start(f32[128,2048]{1,0:T(8,128)} %get-tuple-element.69), channel_id=1, source_target_pairs={{0,8},{1,9},{2,10},{3,11},{4,12},{5,13},{6,14},{7,15},{8,0},{9,1},... | collective-permute-start | bytes 3145736 | tf_op jit(solution)/shard_map/ppermute | solution.py:802
  544.9 41.3 %collective-permute-start.5 = (f32[7,512,1280]{2,1,0:T(8,128)}, f32[7,512,1280]{2,1,0:T(8,128)}, u32[]{:S(2)}, u32[]{:S(2)}) collective-permute-start(f32[7,512,1280]{2,1,0:T(8,128)} %get-tuple-element.74), channel_id=1, source_target_pairs={{0,1},{1,0},{2,3},{3,2},{4,5},{5,4},{6,7},{7,6},{8,9},{9,8},{10,11... | collective-permute-start | bytes 55050248 | tf_op jit(solution)/shard_map/ppermute | solution.py:808
  545.0 41.2 %collective-permute-start.4 = (f32[3,512,1280]{2,1,0:T(8,128)}, f32[3,512,1280]{2,1,0:T(8,128)}, u32[]{:S(2)}, u32[]{:S(2)}) collective-permute-start(f32[3,512,1280]{2,1,0:T(8,128)} %get-tuple-element.73), channel_id=1, source_target_pairs={{0,1},{1,0},{2,3},{3,2},{4,5},{5,4},{6,7},{7,6},{8,9},{9,8},{10,11... | collective-permute-start | bytes 23592968 | tf_op jit(solution)/shard_map/ppermute | solution.py:808
  623.7 6.1 copy-start
  638.0 22.1 %copy-start.5 = (f32[8,2048]{1,0:T(8,128)}, f32[8,2048]{1,0:T(8,128)S(1)}, u32[]{:S(2)}) copy-start(f32[8,2048]{1,0:T(8,128)S(1)} %bitcast_reduce_fusion) | copy-start | bytes 196612
  660.1 5.8 copy-start.1
  665.9 6.3 slice-start
Sparse Core Ops, SparseCore 0:
  92.9 42.9 all-gather.8
  142.2 47.6 all-gather.10
  327.0 85.1 all-gather.16
  414.3 137.2 all-gather.14
  553.7 76.4 all-gather.12
where the time goes:
time: 681 us; the launch traced here: 679 us
  Pallas kernels  581 us (85%)
  waiting for transfers between devices  48.9 us (7%)
  local copies, waits for them, and re-layouts  16.6 us (2%)
  other arithmetic  14.4 us (2%)
  between operations  14.1 us (2%)
    pallas_call x4, Pallas kernels, grad_vocab(): pl.pallas_call(functools.partial(dwv_kernel, lo, hi, counts), out_shape=o...  285 us
    pallas_call x1, Pallas kernels, backward(): pl.pallas_call(bwd_kernel, out_shape=tuple((jax.ShapeDtypeStruct((rows, G...  132 us
    pallas_call x1, Pallas kernels, forward(): pl.pallas_call(fwd_kernel, out_shape=(jax.ShapeDtypeStruct((T, Q, G4), F3...  83.5 us
    ppermute x3, waiting for transfers between devices, local_grads(): swapped.append((SPLITS[i], lax.ppermute(sent, 'data', other_core)))  48.7 us
    pallas_call x1, Pallas kernels, head(): pl.pallas_call(head_kernel, out_shape=(jax.ShapeDtypeStruct((N, H), F32),...  46 us
    pallas_call x3, Pallas kernels, copy_call(): pl.pallas_call(kernel, out_shape=jax.ShapeDtypeStruct(out, F32), in_specs...  34.9 us
    unnamed x18, local copies, waits for them, and re-layouts  15.3 us
  transfers between devices with their start and end apart: 11, of which 2 were waited for; matrix products, arithmetic and copies ran while one was open for 2% of the time, Pallas kernels for 72%

commit v1 on v0

--- a/solution.py
+++ b/solution.py
@@ -20,7 +20,7 @@
 NDEV = 16
 CH = 4
 NR = 6
-PIECES = ((0, 0, 256), (256, 384, 256), (512, 384, 128))
+PIECES = ((0, 0, 256), (256, 384, 352), (608, 384, 32))
 F32 = jnp.float32
 BF16 = jnp.bfloat16
 MESH = pl.DeviceIdType.MESH
@@ -376,7 +376,7 @@
     outs = []
     for i, (dst, (row, step, rows), at) in enumerate(((both, PIECES[0], 0), (give1, PIECES[1], 1 - plane), (give2, PIECES[2], 1 - plane),
                                                       (own1, PIECES[1], plane), (own2, PIECES[2], plane))):
-        outs.append(pltpu.make_async_copy(acc.at[pl.ds(pl.multiple_of(row + at * step, LANE), rows)], dst, osem.at[i]))
+        outs.append(pltpu.make_async_copy(acc.at[pl.ds(pl.multiple_of(row + at * step, R), rows)], dst, osem.at[i]))
         outs[i].start()
     for out in outs:
         out.wait()
@@ -546,6 +546,10 @@
 NOWN = (NVB + 1) // 2
 
 
+def block_of(j, side):
+    return j + side * (NVB - 1 - 2 * j)
+
+
 def dwv_kernel(lo, hi, came, x_hbm, st_ref, w_hbm, *rest):
     nshared = min(hi, NOWN - 1) - lo
     arrived = rest[len(rest) - 15 - 1 - (nshared > 0) - len(came):]
@@ -554,19 +558,16 @@
     xv, xtv, wv, g0, g1, acc, lse, tgt, box, wsem, xsem, osem, gsem, isem, psem = rest[-15:]
     core = lax.rem(lax.axis_index("data"), 2)
 
-    def block(j, side):
-        return j + side * (NVB - 1 - 2 * j)
-
     def cols(b):
         return pl.ds(pl.multiple_of(b * VB, VB), VB)
 
     def wcopy(i):
         buf = lax.rem(i, 2)
-        return pltpu.make_async_copy(w_hbm.at[:, cols(block(lo + i, core))], wv.at[buf], wsem.at[buf])
+        return pltpu.make_async_copy(w_hbm.at[:, cols(block_of(lo + i, core))], wv.at[buf], wsem.at[buf])
 
     def keep(i):
         buf = lax.rem(i, 2)
-        return pltpu.make_async_copy(acc.at[buf], dw_hbm.at[:, cols(block(lo + i, core))], osem.at[buf])
+        return pltpu.make_async_copy(acc.at[buf], dw_hbm.at[:, cols(block_of(lo + i, core))], osem.at[buf])
 
     def give(i):
         buf = lax.rem(i, 2)
@@ -574,12 +575,16 @@
 
     def done(i):
         keep(i).start()
-        if nshared > 0:
+
+        @pl.when(i < nshared)
+        def _():
             give(i).start()
 
     def drained(i):
         keep(i).wait()
-        if nshared > 0:
+
+        @pl.when(i < nshared)
+        def _():
             give(i).wait()
 
     pieces = [(src, first, i, r) for src, (first, count) in zip(arrived, came) for i in range(count) for r in range(0, H, LANE)]
@@ -589,7 +594,7 @@
         return pltpu.make_async_copy(src.at[i, pl.ds(r, LANE)], box.at[k, slot], isem.at[k, slot])
 
     def put(first, i, r, k, slot):
-        return pltpu.make_async_copy(box.at[k, slot], dw_hbm.at[pl.ds(r, LANE), cols(block(first + i, 1 - core))], psem.at[k, slot])
+        return pltpu.make_async_copy(box.at[k, slot], dw_hbm.at[pl.ds(r, LANE), cols(block_of(first + i, 1 - core))], psem.at[k, slot])
 
     def pieces_of(h, act):
         at = 0
@@ -643,7 +648,7 @@
         gnew, gold = ((g0, g1), (g1, g0))[u % 2]
         k, i = lax.rem(it, NK) + u, it // NK
         base = pl.multiple_of(k * TB, TB)
-        lane = lax.broadcasted_iota(jnp.int32, (R, LANE), 1) + block(lo + i, core) * VB
+        lane = lax.broadcasted_iota(jnp.int32, (R, LANE), 1) + block_of(lo + i, core) * VB
         for c in range(0, VB, HB):
             lgt = dot(xv[pl.ds(base, TB), :], wv[lax.rem(i, 2), :, c:c + HB])
             weight(it + u - 1, gold, slice(c, c + HB), u == 1)
@@ -763,6 +768,23 @@
     )(*args)
 
 
+def land_blocks(first, sent, dwv):
+    per = H // LANE
+
+    def kernel(src, _, dst, *scratch):
+        other = 1 - lax.rem(lax.axis_index("data"), 2)
+
+        def rows(i):
+            return pl.ds(pl.multiple_of(lax.rem(i, per) * LANE, LANE), LANE)
+
+        def target(i):
+            return dst.at[rows(i), pl.ds(pl.multiple_of(block_of(first + i // per, other) * VB, VB), VB)]
+
+        copy_ring(sent.shape[0] * per, lambda i: src.at[i // per, rows(i)], target, *scratch)
+
+    return copy_call(kernel, (H, V), (LANE, VB), (sent, dwv))
+
+
 def place_dw(piece, parts, *before):
     row, step, rows = PIECES[piece]
 
@@ -770,14 +792,14 @@
         dst, scratch = rest[-4], rest[-3:]
 
         def target(i):
-            return dst.at[gray(lax.rem(i, S)), pl.ds(pl.multiple_of(row + i // S * step, LANE), rows)]
+            return dst.at[gray(lax.rem(i, S)), pl.ds(pl.multiple_of(row + i // S * step, R), rows)]
 
         copy_ring(parts.shape[0], lambda i: src.at[i, 0:rows], target, *scratch)
 
     return copy_call(kernel, (L, 2 * H, G4), (rows, G4), (parts,) + before)
 
 
-SPLITS = (0, 2, 5, 12, NOWN)
+SPLITS = (0, 2, 6, NOWN)
 
 
 def solution(mesh):
@@ -807,11 +829,12 @@
             gathered.append(lax.all_gather(part, 'data', axis=0, axis_index_groups=None if i else planes))
             swapped.append((SPLITS[i], lax.ppermute(sent, 'data', other_core)))
             dwv = (dwv,)
-        dwv, = grad_vocab(SPLITS[3], SPLITS[4], x_all, stats, w_vocab, dwv, swapped[1:])
         dw = place_dw(0, gathered[0])
+        for first, sent in swapped[1:]:
+            dwv = (land_blocks(first, sent, *dwv),)
         dw = place_dw(2, gathered[2], place_dw(1, gathered[1], dw))
         db = gathered[1][:, PIECES[1][2]:].reshape(NDEV // S, S, R, G4).sum(axis=(0, 2))
         db = jnp.stack([db[gray(i)] for i in range(L)])
-        return dw, db, dwv, jnp.swapaxes(dx, 0, 1)
+        return dw, db, dwv[0], jnp.swapaxes(dx, 0, 1)
 
     return jax.shard_map(local_grads, mesh=mesh, in_specs=(P('data'), P('data'), P(), P(), P()), out_specs=(P(), P(), P(), P('data')), check_vma=False)

time: 681 us -> 686 us (level)
    pallas_call x3 -> x5, Pallas kernels: 34.9 us -> 61.7 us  [copy_call(): pl.pallas_call(kernel, out_shape=jax.ShapeDtypeStruct(out, F32), in_specs...]
    pallas_call x4 -> x3, Pallas kernels: 285 us -> 264 us  [grad_vocab(): pl.pallas_call(functools.partial(dwv_kernel, lo, hi, counts), out_shape=o...]
    ppermute x3, waiting for transfers between devices: 0.01 us -> 12.2 us  [local_grads(): got = lax.ppermute(give, 'data', other_plane)]
    ppermute x3, waiting for transfers between devices: 48.7 us -> 39.8 us  [local_grads(): swapped.append((SPLITS[i], lax.ppermute(sent, 'data', other_core)))]
    unnamed x18 -> x20, local copies, waits for them, and re-layouts: 15.3 us -> 11.5 us
  transfers between devices with their start and end apart: 11 -> 11, of which waited for: 2 -> 3; matrix products, arithmetic and copies ran while one was open for 2% -> 2% of each run, Pallas kernels for 72% -> 73%
where the time goes in v1:
time: 686 us; the launch traced here: 684 us
  Pallas kernels  587 us (86%)
  waiting for transfers between devices  52.2 us (8%)
  between operations  14.1 us (2%)
  other arithmetic  13.8 us (2%)
  local copies, waits for them, and re-layouts  12.8 us (2%)
    pallas_call x3, Pallas kernels, grad_vocab(): pl.pallas_call(functools.partial(dwv_kernel, lo, hi, counts), out_shape=o...  264 us
    pallas_call x1, Pallas kernels, backward(): pl.pallas_call(bwd_kernel, out_shape=tuple((jax.ShapeDtypeStruct((rows, G...  132 us
    pallas_call x1, Pallas kernels, forward(): pl.pallas_call(fwd_kernel, out_shape=(jax.ShapeDtypeStruct((T, Q, G4), F3...  83.5 us
    pallas_call x5, Pallas kernels, copy_call(): pl.pallas_call(kernel, out_shape=jax.ShapeDtypeStruct(out, F32), in_specs...  61.7 us
    pallas_call x1, Pallas kernels, head(): pl.pallas_call(head_kernel, out_shape=(jax.ShapeDtypeStruct((N, H), F32),...  46 us
    ppermute x3, waiting for transfers between devices, local_grads(): swapped.append((SPLITS[i], lax.ppermute(sent, 'data', other_core)))  39.8 us
  transfers between devices with their start and end apart: 11, of which 3 were waited for; matrix products, arithmetic and copies ran while one was open for 2% of the time, Pallas kernels for 73%

profile of v1, /device:TPU:0, one launch (start us, length us, event | category | flops | bytes accessed | tf_op | source)
XLA Modules:
  0.0 683.9 jit_solution(14668689262151017368)
XLA Ops:
  7.2 0.0 all-gather.9.cloned.1.call-start
  7.2 1.2 copy.29
  8.4 0.8 copy-done.2
  9.3 83.5 %lstm_fwd.1 = (f32[48,64,2048]{2,1,0:T(8,128)}, f32[48,64,512]{2,1,0:T(8,128)}, bf16[48,64,512]{2,1,0:T(8,128)(2,1)}, bf16[48,8,8,512]{3,2,1,0:T(8,128)(2,1)}, bf16[48,8,512]{2,1,0:T(8,128)(2,1)}) custom-call(bf16[48,8,512]{2,1,0:T(8,128)(2,1)S(1)} %bitcast.15, bf16[8,1024,2048]{2,1,0:T(8,128)(2,1)} %w_hbm.8, f32[8,2048]{1,0:T(8,128)S(1)} %copy-done.2), custom_call_target="tpu_custom_call" | custom-call | flops 60000002048 | bytes 80000000 | tf_op jit(solution)/shard_map/lstm_fwd/pallas_call | solution.py:207
  92.8 0.0 all-gather.11.cloned.1.call-start
  92.8 0.1 copy.24
  92.9 0.8 reshape.33.t_ref
  93.7 0.1 copy.26
  93.8 0.1 convert_element_type.12
  93.9 46.0 %head.1 = (f32[384,512]{1,0:T(8,128)}, f32[384,1]{1,0:T(8,128)}) custom-call(bf16[384,512]{1,0:T(8,128)(2,1)} %bitcast.1.x_ref, s32[384,1]{1,0:T(8,128)} %reshape.33.t_ref, bf16[512,32000]{1,0:T(8,128)(2,1)} %w_hbm.11), custom_call_target="tpu_custom_call" | custom-call | flops 40000000000 | bytes 70000000 | tf_op jit(solution)/shard_map/head/pallas_call | solution.py:529
  139.9 1.1 reduce.2
  141.0 0.1 broadcast_in_dim.13
  141.1 0.1 broadcast_in_dim.14
  141.2 0.8 pad_maximum_fusion.1
  142.0 0.0 all-gather.17.cloned.1.call-start
  142.1 0.0 all-gather.9.cloned.1.call-done.x_hbm
  142.1 131.9 %lstm_bwd.1 = (f32[256,2048]{1,0:T(8,128)}, f32[352,2048]{1,0:T(8,128)}, f32[32,2048]{1,0:T(8,128)}, f32[352,2048]{1,0:T(8,128)}, f32[32,2048]{1,0:T(8,128)}, /*index=5*/f32[8,2048]{1,0:T(8,128)}, f32[48,8,512]{2,1,0:T(8,128)}) custom-call(f32[48,8,512]{2,1,0:T(8,128)} %bitcast.20, f32[48,64,2048]{2,1,0:T(8,128)} %get-tuple-element.43.gates_hbm, ...), custom_call_target="tpu_custom_call" | custom-call | flops 109999996928 | bytes 80000000 | tf_op jit(solution)/shard_map/lstm_bwd/pallas_call | solution.py:401
  274.0 1.5 collective-permute-start
  275.5 47.2 %dwv.3 = (f32[512,32000]{1,0:T(8,128)}, f32[2,512,1280]{2,1,0:T(8,128)}) custom-call(bf16[6144,512]{1,0:T(8,128)(2,1)} %all-gather.9.cloned.1.call-done.x_hbm, f32[6144,128]{1,0:T(8,128)} %all-gather.11.cloned.1.call-done.st_ref, bf16[512,32000]{1,0:T(8,128)(2,1)} %w_hbm.11), custom_call_target="tpu_custom_call" | custom-call | flops 40000000000 | bytes 100000000 | tf_op jit(solution)/shard_map/dwv/pallas_call | solution.py:708
  322.7 3.9 add.9
  326.7 0.0 all-gather.15.cloned.1.call-start
  326.7 0.6 collective-permute-start.1
  327.3 82.4 %dwv.4 = (f32[512,32000]{1,0:T(8,128)}, f32[4,512,1280]{2,1,0:T(8,128)}) custom-call(bf16[6144,512]{1,0:T(8,128)(2,1)} %all-gather.9.cloned.1.call-done.x_hbm, f32[6144,128]{1,0:T(8,128)} %all-gather.11.cloned.1.call-done.st_ref, bf16[512,32000]{1,0:T(8,128)(2,1)} %w_hbm.11, f32[512,32000]{1,0:T(8,128)} %get-tuple-element.55.rest_0_), custom_call_target="tpu_custom_call", output_to_operand_aliasing={{0}: (3, {})} | custom-call | flops 80000000000 | bytes 100000000 | tf_op jit(solution)/shard_map/dwv/pallas_call | solution.py:708
  409.7 3.4 add.10
  413.2 1.8 pad_maximum_fusion
  414.9 0.3 all-gather.13.cloned.1.call-start
  415.2 0.0 collective-permute-start.2
  415.3 9.0 %collective-permute-done.2.rest_1_ = f32[2,512,1280]{2,1,0:T(8,128)} collective-permute-done((f32[2,512,1280]{2,1,0:T(8,128)}, f32[2,512,1280]{2,1,0:T(8,128)}, u32[]{:S(2)}, u32[]{:S(2)}) %collective-permute-start.2) | collective-permute-done | bytes 5242912 | tf_op jit(solution)/shard_map/ppermute | solution.py:830
  424.3 134.3 %dwv.5 = (f32[512,32000]{1,0:T(8,128)}, f32[6,512,1280]{2,1,0:T(8,128)}) custom-call(bf16[6144,512]{1,0:T(8,128)(2,1)} %all-gather.9.cloned.1.call-done.x_hbm, f32[6144,128]{1,0:T(8,128)} %all-gather.11.cloned.1.call-done.st_ref, bf16[512,32000]{1,0:T(8,128)(2,1)} %w_hbm.11, ...), custom_call_target="tpu_custom_call", output_to_operand_aliasing={{0}: (3, {})} | custom-call | flops 140000002048 | bytes 100000000 | tf_op jit(solution)/shard_map/dwv/pallas_call | solution.py:708
  558.6 0.3 collective-permute-start.4
  558.8 0.3 collective-permute-start.5
  559.1 1.1 collective-permute-start.3
  560.2 1.3 copy.27
  561.5 12.2 %collective-permute-done.3 = f32[32,2048]{1,0:T(8,128)S(1)} collective-permute-done((f32[32,2048]{1,0:T(8,128)S(1)}, f32[32,2048]{1,0:T(8,128)S(1)}, u32[]{:S(2)}, u32[]{:S(2)}) %collective-permute-start.3) | collective-permute-done | bytes 262176 | tf_op jit(solution)/shard_map/ppermute | solution.py:824
  573.7 0.7 add.11
  574.5 30.8 %collective-permute-done.5.src = f32[4,512,1280]{2,1,0:T(8,128)} collective-permute-done((f32[4,512,1280]{2,1,0:T(8,128)}, f32[4,512,1280]{2,1,0:T(8,128)}, u32[]{:S(2)}, u32[]{:S(2)}) %collective-permute-start.5) | collective-permute-done | bytes 10485792 | tf_op jit(solution)/shard_map/ppermute | solution.py:830
  605.3 9.0 %shard_map.87._ = f32[512,32000]{1,0:T(8,128)} custom-call(f32[4,512,1280]{2,1,0:T(8,128)} %collective-permute-done.5.src, f32[512,32000]{1,0:T(8,128)} %get-tuple-element.74._), custom_call_target="tpu_custom_call", output_to_operand_aliasing={{}: (1, {})} | custom-call | flops 20000000000 | bytes 130000000 | tf_op jit(solution)/shard_map/pallas_call | solution.py:759
  614.4 12.1 %shard_map.88 = f32[512,32000]{1,0:T(8,128)} custom-call(f32[6,512,1280]{2,1,0:T(8,128)} %collective-permute-done.4.src, f32[512,32000]{1,0:T(8,128)} %shard_map.87._), custom_call_target="tpu_custom_call", output_to_operand_aliasing={{}: (1, {})} | custom-call | flops 20000000000 | bytes 130000000 | tf_op jit(solution)/shard_map/pallas_call | solution.py:759
  626.5 0.0 all-gather.17.cloned.1.call-done
  626.5 5.9 copy-done
  632.4 6.6 shard_map.84.rest_0_
  638.9 0.0 all-gather.15.cloned.1.call-done
  639.0 1.5 slice_reduce_fusion
  640.5 30.9 %shard_map.85.rest_0_ = f32[8,1024,2048]{2,1,0:T(8,128)} custom-call(f32[16,360,2048]{2,1,0:T(8,128)} %bitcast.17, f32[8,1024,2048]{2,1,0:T(8,128)} %shard_map.84.rest_0_), custom_call_target="tpu_custom_call", output_to_operand_aliasing={{}: (1, {})} | custom-call | flops 20000000000 | bytes 130000000 | tf_op jit(solution)/shard_map/pallas_call | solution.py:759
  671.4 0.0 all-gather.13.cloned.1.call-done
  671.4 2.2 copy-done.1
  673.6 3.1 shard_map.86
  676.8 0.7 pad_maximum_fusion.2
  (29 shorter events, 0.2 us)
Async XLA Ops:
  7.2 134.9 %all-gather.9.cloned.1.call-start = ((), (), s32[]{:S(2)}) async-start(), calls=%async_computation | async-start | bytes 6684672 | tf_op jit(solution)/shard_map/all_gather | solution.py:813
  8.4 0.8 copy-start.2
  9.3 83.5 %copy-start.7 = (s32[8,48]{1,0:T(8,128)S(1)}, s32[8,48]{1,0:T(8,128)}, u32[]{:S(2)}) copy-start(s32[8,48]{1,0:T(8,128)} %param.6) | copy-start | bytes 4612
  92.8 182.8 %all-gather.11.cloned.1.call-start = ((), (), s32[]{:S(2)}) async-start(), calls=%async_computation.1 | async-start | bytes 3342336 | tf_op jit(solution)/shard_map/all_gather | solution.py:814
  142.0 484.4 %all-gather.17.cloned.1.call-start = ((), (), s32[]{:S(2)}) async-start(), calls=%async_computation.4 | async-start | bytes 18874368 | tf_op jit(solution)/shard_map/all_gather | solution.py:829
  274.0 48.7 %collective-permute-start = (f32[256,2048]{1,0:T(8,128)}, f32[256,2048]{1,0:T(8,128)}, u32[]{:S(2)}, u32[]{:S(2)}) collective-permute-start(f32[256,2048]{1,0:T(8,128)} %get-tuple-element.53), channel_id=1, source_target_pairs={{0,8},{1,9},{2,10},{3,11},{4,12},{5,13},{6,14},{7,15},{8,0},{9,1},... | collective-permute-start | bytes 6291464 | tf_op jit(solution)/shard_map/ppermute | solution.py:824
  326.7 312.3 %all-gather.15.cloned.1.call-start = ((), (), s32[]{:S(2)}) async-start(), calls=%async_computation.3 | async-start | bytes 50135040 | tf_op jit(solution)/shard_map/all_gather | solution.py:829
  326.7 83.0 %collective-permute-start.1 = (f32[352,2048]{1,0:T(8,128)}, f32[352,2048]{1,0:T(8,128)}, u32[]{:S(2)}, u32[]{:S(2)}) collective-permute-start(f32[352,2048]{1,0:T(8,128)} %get-tuple-element.60), channel_id=1, source_target_pairs={{0,8},{1,9},{2,10},{3,11},{4,12},{5,13},{6,14},{7,15},{8,0},{9,1},... | collective-permute-start | bytes 8650760 | tf_op jit(solution)/shard_map/ppermute | solution.py:824
  409.7 3.4 copy-start.6
  414.9 256.5 %all-gather.13.cloned.1.call-start = ((), (), s32[]{:S(2)}) async-start(), calls=%async_computation.2 | async-start | bytes 4456448 | tf_op jit(solution)/shard_map/all_gather | solution.py:829
  415.2 143.9 %copy-start.8 = (f32[32,2048]{1,0:T(8,128)S(1)}, f32[32,2048]{1,0:T(8,128)}, u32[]{:S(2)}) copy-start(f32[32,2048]{1,0:T(8,128)} %get-tuple-element.69) | copy-start | bytes 786436
  415.2 144.9 %copy-start.3 = (f32[48,8,512]{2,1,0:T(8,128)S(1)}, f32[48,8,512]{2,1,0:T(8,128)}, u32[]{:S(2)}) copy-start(f32[48,8,512]{2,1,0:T(8,128)} %get-tuple-element.75) | copy-start | bytes 2359300
  415.2 158.5 %copy-start.4 = (f32[32,2048]{1,0:T(8,128)S(1)}, f32[32,2048]{1,0:T(8,128)}, u32[]{:S(2)}) copy-start(f32[32,2048]{1,0:T(8,128)} %get-tuple-element.66) | copy-start | bytes 786436
  415.2 9.0 %collective-permute-start.2 = (f32[2,512,1280]{2,1,0:T(8,128)}, f32[2,512,1280]{2,1,0:T(8,128)}, u32[]{:S(2)}, u32[]{:S(2)}) collective-permute-start(f32[2,512,1280]{2,1,0:T(8,128)} %get-tuple-element.64), channel_id=1, source_target_pairs={{0,1},{1,0},{2,3},{3,2},{4,5},{5,4},{6,7},{7,6},{8,9},{9,8},{10,11... | collective-permute-start | bytes 15728648 | tf_op jit(solution)/shard_map/ppermute | solution.py:830
  558.6 55.8 %collective-permute-start.4 = (f32[6,512,1280]{2,1,0:T(8,128)}, f32[6,512,1280]{2,1,0:T(8,128)}, u32[]{:S(2)}, u32[]{:S(2)}) collective-permute-start(f32[6,512,1280]{2,1,0:T(8,128)} %get-tuple-element.72), channel_id=1, source_target_pairs={{0,1},{1,0},{2,3},{3,2},{4,5},{5,4},{6,7},{7,6},{8,9},{9,8},{10,11... | collective-permute-start | bytes 47185928 | tf_op jit(solution)/shard_map/ppermute | solution.py:830
  558.8 46.5 %collective-permute-start.5 = (f32[4,512,1280]{2,1,0:T(8,128)}, f32[4,512,1280]{2,1,0:T(8,128)}, u32[]{:S(2)}, u32[]{:S(2)}) collective-permute-start(f32[4,512,1280]{2,1,0:T(8,128)} %get-tuple-element.73), channel_id=1, source_target_pairs={{0,1},{1,0},{2,3},{3,2},{4,5},{5,4},{6,7},{7,6},{8,9},{9,8},{10,11... | collective-permute-start | bytes 31457288 | tf_op jit(solution)/shard_map/ppermute | solution.py:830
  559.1 14.6 %collective-permute-start.3 = (f32[32,2048]{1,0:T(8,128)S(1)}, f32[32,2048]{1,0:T(8,128)S(1)}, u32[]{:S(2)}, u32[]{:S(2)}) collective-permute-start(f32[32,2048]{1,0:T(8,128)S(1)} %copy-done.8), channel_id=1, source_target_pairs={{0,8},{1,9},{2,10},{3,11},{4,12},{5,13},{6,14},{7,15},{8,0},{9,1},... | collective-permute-start | bytes 786440 | tf_op jit(solution)/shard_map/ppermute | solution.py:824
  626.5 5.9 copy-start
  640.5 30.9 %copy-start.5 = (f32[8,2048]{1,0:T(8,128)}, f32[8,2048]{1,0:T(8,128)S(1)}, u32[]{:S(2)}) copy-start(f32[8,2048]{1,0:T(8,128)S(1)} %bitcast_reduce_fusion) | copy-start | bytes 196612
  671.4 2.2 copy-start.1
  673.6 3.1 slice-start
Sparse Core Ops, SparseCore 0:
  92.9 42.9 all-gather.8
  142.2 47.6 all-gather.10
  326.8 85.3 all-gather.16
  415.1 184.2 all-gather.14
  601.4 35.3 all-gather.12

commit v2 on v1

--- a/solution.py
+++ b/solution.py
@@ -298,13 +298,8 @@
     lax.fori_loop(0, G4 // HB, turn, 0)
 
     def weight():
-        def part(k, _):
-            for n in range(0, 2 * H, HB):
-                cols = pl.ds(pl.multiple_of(k * 2 * H + n, HB), HB)
-                acc[:, cols] += dot(ut[...], dall[:, cols])
-            return 0
-
-        lax.fori_loop(0, G4 // (2 * H), part, 0)
+        for n in range(0, G4, HB):
+            acc[:, n:n + HB] += dot(ut[...], dall[:, n:n + HB])
 
     def two(n, state):
         p = T // 2 - 1 - n
@@ -416,6 +411,7 @@
 VB = 1280
 NVB = V // VB
 N = T * R
+CHUNKS = ((0, 512), (512, 512), (1024, 256))
 NW = 4
 RB = 64
 
@@ -437,44 +433,35 @@
     sm[...] = jnp.zeros(sm.shape, F32)
     dx_ref[...] = jnp.zeros(dx_ref.shape, F32)
 
-    def each(n, act):
-        lax.fori_loop(0, n, lambda i, _: (act(i), 0)[1], 0)
-
-    def at(i, size):
-        return pl.ds(pl.multiple_of(i * size, size), size)
-
-    def logits(b, cols):
-        lg[b, :, cols] = dot(x_ref[...], wv[lax.rem(b, NW), :, cols])
-
-    def sums(b, rows):
-        m_old = mx[rows, :]
-        m_new = m_old
-        for c in range(0, VB, LANE):
-            m_new = jnp.maximum(m_new, lg[b, rows, c:c + LANE])
-        acc = sm[rows, :] * jnp.exp(m_old - m_new)
-        for c in range(0, VB, LANE):
-            acc = acc + jnp.exp(lg[b, rows, c:c + LANE] - m_new)
-        mx[rows, :] = m_new
-        sm[rows, :] = acc
+    def logits(b, c, size):
+        part = dot(x_ref[...], wv[lax.rem(b, NW), :, c:c + size])
+        lg[b, :, c:c + size] = part
+        for r in range(0, N, RB):
+            rows = slice(r, r + RB)
+            vals = [part[rows, h:h + LANE] for h in range(0, size, LANE)]
+            m_old = mx[rows, :]
+            m_new = functools.reduce(jnp.maximum, vals, m_old)
+            mx[rows, :] = m_new
+            sm[rows, :] = functools.reduce(jnp.add, [jnp.exp(v - m_new) for v in vals], sm[rows, :] * jnp.exp(m_old - m_new))
+
+    def block(b):
+        for c, size in CHUNKS:
+            logits(b, c, size)
 
     wcopy(0).wait()
-    each(VB // HB, lambda c: logits(0, at(c, HB)))
+    block(0)
 
     def first(h, _):
         b = 2 * h + 1
         ready(b)
         for i in range(2):
-            for c in range(0, VB, HB):
-                logits(b + i, slice(c, c + HB))
-            for r in range(0, N, RB):
-                sums(b + i - 1, slice(r, r + RB))
+            block(b + i)
         return 0
 
     lax.fori_loop(0, NVB // 2, first, 0)
-    each(N // RB, lambda r: sums(NVB - 1, at(r, RB)))
 
     def finish(r):
-        rows = at(r, LANE)
+        rows = slice(r, r + LANE)
         top = jnp.max(mx[rows, :], axis=1, keepdims=True)
         tot = jnp.sum(sm[rows, :] * jnp.exp(mx[rows, :] - top), axis=1, keepdims=True)
         lse = top + jnp.log(tot)
@@ -482,7 +469,8 @@
         mx[rows, :] = jnp.broadcast_to(lse, (LANE, LANE))
         tb[rows, :] = jnp.broadcast_to(t_ref[rows, :], (LANE, LANE))
 
-    each(N // LANE, finish)
+    for r in range(0, N, LANE):
+        finish(r)
 
     def grads(b, gb, c):
         ids = [b * VB + c + h + lax.broadcasted_iota(jnp.int32, (RB, LANE), 1) for h in (0, LANE)]
@@ -497,7 +485,8 @@
     def apply(b, gb, cols):
         return dot_tt(gb[:, cols], wv[lax.rem(b + NVB, NW), :, cols])
 
-    each(VB // HB, lambda c: grads(0, g0, pl.multiple_of(c * HB, HB)))
+    for c in range(0, VB, HB):
+        grads(0, g0, c)
 
     def second(h, _):
         for i in range(2):
@@ -518,11 +507,8 @@
 
     lax.fori_loop(0, NVB // 2, second, 0)
     wcopy(2 * NVB - 1).wait()
-
-    def last(c):
-        dx_ref[...] += apply(NVB - 1, g0, at(c, HB))
-
-    each(VB // HB, last)
+    for c in range(0, VB, HB):
+        dx_ref[...] += apply(NVB - 1, g0, slice(c, c + HB))
 
 
 def head(x, tgt, w_vocab):
@@ -622,11 +608,16 @@
 
     n = hi - lo
     wcopy(0).start()
-    cx = pltpu.make_async_copy(x_hbm, xv, xsem.at[0])
-    cx.start()
-    cx.wait()
+
+    def xcopy(k):
+        rows = pl.ds(k * TB, TB)
+        return pltpu.make_async_copy(x_hbm.at[rows], xv.at[rows], xsem.at[k])
+
+    for k in range(NK):
+        xcopy(k).start()
 
     def turn(k, _):
+        xcopy(k).wait()
         for c in range(0, TB, HB):
             rows = pl.ds(pl.multiple_of(k * TB + c, HB), HB)
             xtv[k, :, c:c + HB] = xv[rows, :].T
@@ -714,7 +705,7 @@
         scratch_shapes=[pltpu.VMEM((NTOK, H), BF16), pltpu.VMEM((NK, H, TB), BF16), pltpu.VMEM((2, H, VB), BF16)]
         + [pltpu.VMEM((TB, VB), BF16)] * 2
         + [pltpu.VMEM((2, H, VB), F32)] + [pltpu.VMEM((NTOK, LANE), F32)] * 2 + [pltpu.VMEM((2, per, LANE, VB), F32)]
-        + [DMA((2,)), DMA((1,)), DMA((2,)), DMA((2,)), DMA((2, per)), DMA((2, per))],
+        + [DMA((2,)), DMA((NK,)), DMA((2,)), DMA((2,)), DMA((2, per)), DMA((2, per))],
         compiler_params=pltpu.CompilerParams(vmem_limit_bytes=62 * MIB),
         cost_estimate=pl.CostEstimate(flops=(hi - lo) * 20_000_000_000, bytes_accessed=100_000_000, transcendentals=0),
         name="dwv",

time: 686 us -> 676 us (0.985)
  Pallas kernels: 587 us -> 575 us
where the time goes in v2:
time: 676 us; the launch traced here: 673 us
  Pallas kernels  575 us (85%)
  waiting for transfers between devices  52.8 us (8%)
  between operations  14.1 us (2%)
  other arithmetic  13.6 us (2%)
  local copies, waits for them, and re-layouts  12.8 us (2%)
    pallas_call x3, Pallas kernels, grad_vocab(): pl.pallas_call(functools.partial(dwv_kernel, lo, hi, counts), out_shape=o...  259 us
    pallas_call x1, Pallas kernels, backward(): pl.pallas_call(bwd_kernel, out_shape=tuple((jax.ShapeDtypeStruct((rows, G...  129 us
    pallas_call x1, Pallas kernels, forward(): pl.pallas_call(fwd_kernel, out_shape=(jax.ShapeDtypeStruct((T, Q, G4), F3...  83.5 us
    pallas_call x5, Pallas kernels, copy_call(): pl.pallas_call(kernel, out_shape=jax.ShapeDtypeStruct(out, F32), in_specs...  61.5 us
    pallas_call x1, Pallas kernels, head(): pl.pallas_call(head_kernel, out_shape=(jax.ShapeDtypeStruct((N, H), F32),...  43.2 us
    ppermute x3, waiting for transfers between devices, local_grads(): swapped.append((SPLITS[i], lax.ppermute(sent, 'data', other_core)))  40.8 us
  transfers between devices with their start and end apart: 11, of which 3 were waited for; matrix products, arithmetic and copies ran while one was open for 2% of the time, Pallas kernels for 73%

profile of v2, /device:TPU:0, one launch (start us, length us, event | category | flops | bytes accessed | tf_op | source)
XLA Modules:
  0.0 673.1 jit_solution(1701068794852787623)
XLA Ops:
  7.2 0.0 all-gather.9.cloned.1.call-start
  7.2 1.2 copy.29
  8.4 0.8 copy-done.2
  9.3 83.5 %lstm_fwd.1 = (f32[48,64,2048]{2,1,0:T(8,128)}, f32[48,64,512]{2,1,0:T(8,128)}, bf16[48,64,512]{2,1,0:T(8,128)(2,1)}, bf16[48,8,8,512]{3,2,1,0:T(8,128)(2,1)}, bf16[48,8,512]{2,1,0:T(8,128)(2,1)}) custom-call(bf16[48,8,512]{2,1,0:T(8,128)(2,1)S(1)} %bitcast.15, bf16[8,1024,2048]{2,1,0:T(8,128)(2,1)} %w_hbm.8, f32[8,2048]{1,0:T(8,128)S(1)} %copy-done.2), custom_call_target="tpu_custom_call" | custom-call | flops 60000002048 | bytes 80000000 | tf_op jit(solution)/shard_map/lstm_fwd/pallas_call | solution.py:207
  92.8 0.0 all-gather.11.cloned.1.call-start
  92.8 0.1 copy.24
  92.9 0.8 reshape.33.t_ref
  93.7 0.1 copy.26
  93.8 0.1 convert_element_type.12
  93.9 43.2 %head.1 = (f32[384,512]{1,0:T(8,128)}, f32[384,1]{1,0:T(8,128)}) custom-call(bf16[384,512]{1,0:T(8,128)(2,1)} %bitcast.1.x_ref, s32[384,1]{1,0:T(8,128)} %reshape.33.t_ref, bf16[512,32000]{1,0:T(8,128)(2,1)} %w_hbm.11), custom_call_target="tpu_custom_call" | custom-call | flops 40000000000 | bytes 70000000 | tf_op jit(solution)/shard_map/head/pallas_call | solution.py:515
  137.0 1.1 reduce.2
  138.1 0.1 broadcast_in_dim.13
  138.2 0.1 broadcast_in_dim.14
  138.4 0.8 pad_maximum_fusion.1
  139.2 0.0 all-gather.17.cloned.1.call-start
  139.2 0.0 all-gather.9.cloned.1.call-done.x_hbm
  139.3 128.6 %lstm_bwd.1 = (f32[256,2048]{1,0:T(8,128)}, f32[352,2048]{1,0:T(8,128)}, f32[32,2048]{1,0:T(8,128)}, f32[352,2048]{1,0:T(8,128)}, f32[32,2048]{1,0:T(8,128)}, /*index=5*/f32[8,2048]{1,0:T(8,128)}, f32[48,8,512]{2,1,0:T(8,128)}) custom-call(f32[48,8,512]{2,1,0:T(8,128)} %bitcast.20, f32[48,64,2048]{2,1,0:T(8,128)} %get-tuple-element.43.gates_hbm, ...), custom_call_target="tpu_custom_call" | custom-call | flops 109999996928 | bytes 80000000 | tf_op jit(solution)/shard_map/lstm_bwd/pallas_call | solution.py:396
  267.8 1.5 collective-permute-start
  269.3 45.6 %dwv.3 = (f32[512,32000]{1,0:T(8,128)}, f32[2,512,1280]{2,1,0:T(8,128)}) custom-call(bf16[6144,512]{1,0:T(8,128)(2,1)} %all-gather.9.cloned.1.call-done.x_hbm, f32[6144,128]{1,0:T(8,128)} %all-gather.11.cloned.1.call-done.st_ref, bf16[512,32000]{1,0:T(8,128)(2,1)} %w_hbm.11), custom_call_target="tpu_custom_call" | custom-call | flops 40000000000 | bytes 100000000 | tf_op jit(solution)/shard_map/dwv/pallas_call | solution.py:699
  315.0 3.9 add.9
  318.9 0.0 all-gather.15.cloned.1.call-start
  318.9 0.6 collective-permute-start.1
  319.5 80.0 %dwv.4 = (f32[512,32000]{1,0:T(8,128)}, f32[4,512,1280]{2,1,0:T(8,128)}) custom-call(bf16[6144,512]{1,0:T(8,128)(2,1)} %all-gather.9.cloned.1.call-done.x_hbm, f32[6144,128]{1,0:T(8,128)} %all-gather.11.cloned.1.call-done.st_ref, bf16[512,32000]{1,0:T(8,128)(2,1)} %w_hbm.11, f32[512,32000]{1,0:T(8,128)} %get-tuple-element.55.rest_0_), custom_call_target="tpu_custom_call", output_to_operand_aliasing={{0}: (3, {})} | custom-call | flops 80000000000 | bytes 100000000 | tf_op jit(solution)/shard_map/dwv/pallas_call | solution.py:699
  399.6 3.2 add.10
  402.8 1.8 pad_maximum_fusion
  404.5 0.3 all-gather.13.cloned.1.call-start
  404.8 0.0 collective-permute-start.2
  404.9 9.3 %collective-permute-done.2.rest_1_ = f32[2,512,1280]{2,1,0:T(8,128)} collective-permute-done((f32[2,512,1280]{2,1,0:T(8,128)}, f32[2,512,1280]{2,1,0:T(8,128)}, u32[]{:S(2)}, u32[]{:S(2)}) %collective-permute-start.2) | collective-permute-done | bytes 5242912 | tf_op jit(solution)/shard_map/ppermute | solution.py:821
  414.2 132.9 %dwv.5 = (f32[512,32000]{1,0:T(8,128)}, f32[6,512,1280]{2,1,0:T(8,128)}) custom-call(bf16[6144,512]{1,0:T(8,128)(2,1)} %all-gather.9.cloned.1.call-done.x_hbm, f32[6144,128]{1,0:T(8,128)} %all-gather.11.cloned.1.call-done.st_ref, bf16[512,32000]{1,0:T(8,128)(2,1)} %w_hbm.11, ...), custom_call_target="tpu_custom_call", output_to_operand_aliasing={{0}: (3, {})} | custom-call | flops 140000002048 | bytes 100000000 | tf_op jit(solution)/shard_map/dwv/pallas_call | solution.py:699
  547.1 0.4 collective-permute-start.4
  547.5 0.1 collective-permute-start.5
  547.7 1.4 collective-permute-start.3
  549.1 1.3 copy.27
  550.4 11.9 %collective-permute-done.3 = f32[32,2048]{1,0:T(8,128)S(1)} collective-permute-done((f32[32,2048]{1,0:T(8,128)S(1)}, f32[32,2048]{1,0:T(8,128)S(1)}, u32[]{:S(2)}, u32[]{:S(2)}) %collective-permute-start.3) | collective-permute-done | bytes 262176 | tf_op jit(solution)/shard_map/ppermute | solution.py:815
  562.3 0.7 add.11
  563.1 31.5 %collective-permute-done.5.src = f32[4,512,1280]{2,1,0:T(8,128)} collective-permute-done((f32[4,512,1280]{2,1,0:T(8,128)}, f32[4,512,1280]{2,1,0:T(8,128)}, u32[]{:S(2)}, u32[]{:S(2)}) %collective-permute-start.5) | collective-permute-done | bytes 10485792 | tf_op jit(solution)/shard_map/ppermute | solution.py:821
  594.6 9.0 %shard_map.87._ = f32[512,32000]{1,0:T(8,128)} custom-call(f32[4,512,1280]{2,1,0:T(8,128)} %collective-permute-done.5.src, f32[512,32000]{1,0:T(8,128)} %get-tuple-element.74._), custom_call_target="tpu_custom_call", output_to_operand_aliasing={{}: (1, {})} | custom-call | flops 20000000000 | bytes 130000000 | tf_op jit(solution)/shard_map/pallas_call | solution.py:750
  603.6 12.1 %shard_map.88 = f32[512,32000]{1,0:T(8,128)} custom-call(f32[6,512,1280]{2,1,0:T(8,128)} %collective-permute-done.4.src, f32[512,32000]{1,0:T(8,128)} %shard_map.87._), custom_call_target="tpu_custom_call", output_to_operand_aliasing={{}: (1, {})} | custom-call | flops 20000000000 | bytes 130000000 | tf_op jit(solution)/shard_map/pallas_call | solution.py:750
  615.7 0.0 all-gather.17.cloned.1.call-done
  615.7 5.9 copy-done
  621.6 6.6 shard_map.84.rest_0_
  628.2 0.0 all-gather.15.cloned.1.call-done
  628.2 1.5 slice_reduce_fusion
  629.8 30.8 %shard_map.85.rest_0_ = f32[8,1024,2048]{2,1,0:T(8,128)} custom-call(f32[16,360,2048]{2,1,0:T(8,128)} %bitcast.17, f32[8,1024,2048]{2,1,0:T(8,128)} %shard_map.84.rest_0_), custom_call_target="tpu_custom_call", output_to_operand_aliasing={{}: (1, {})} | custom-call | flops 20000000000 | bytes 130000000 | tf_op jit(solution)/shard_map/pallas_call | solution.py:750
  660.6 0.0 all-gather.13.cloned.1.call-done
  660.6 2.2 copy-done.1
  662.8 3.1 shard_map.86
  665.9 0.7 pad_maximum_fusion.2
  (29 shorter events, 0.2 us)
Async XLA Ops:
  7.2 132.1 %all-gather.9.cloned.1.call-start = ((), (), s32[]{:S(2)}) async-start(), calls=%async_computation | async-start | bytes 6684672 | tf_op jit(solution)/shard_map/all_gather | solution.py:804
  8.4 0.8 copy-start.2
  9.3 83.5 %copy-start.7 = (s32[8,48]{1,0:T(8,128)S(1)}, s32[8,48]{1,0:T(8,128)}, u32[]{:S(2)}) copy-start(s32[8,48]{1,0:T(8,128)} %param.6) | copy-start | bytes 4612
  92.8 176.6 %all-gather.11.cloned.1.call-start = ((), (), s32[]{:S(2)}) async-start(), calls=%async_computation.1 | async-start | bytes 3342336 | tf_op jit(solution)/shard_map/all_gather | solution.py:805
  139.2 476.5 %all-gather.17.cloned.1.call-start = ((), (), s32[]{:S(2)}) async-start(), calls=%async_computation.4 | async-start | bytes 18874368 | tf_op jit(solution)/shard_map/all_gather | solution.py:820
  267.8 47.1 %collective-permute-start = (f32[256,2048]{1,0:T(8,128)}, f32[256,2048]{1,0:T(8,128)}, u32[]{:S(2)}, u32[]{:S(2)}) collective-permute-start(f32[256,2048]{1,0:T(8,128)} %get-tuple-element.53), channel_id=1, source_target_pairs={{0,8},{1,9},{2,10},{3,11},{4,12},{5,13},{6,14},{7,15},{8,0},{9,1},... | collective-permute-start | bytes 6291464 | tf_op jit(solution)/shard_map/ppermute | solution.py:815
  318.9 309.3 %all-gather.15.cloned.1.call-start = ((), (), s32[]{:S(2)}) async-start(), calls=%async_computation.3 | async-start | bytes 50135040 | tf_op jit(solution)/shard_map/all_gather | solution.py:820
  318.9 80.6 %collective-permute-start.1 = (f32[352,2048]{1,0:T(8,128)}, f32[352,2048]{1,0:T(8,128)}, u32[]{:S(2)}, u32[]{:S(2)}) collective-permute-start(f32[352,2048]{1,0:T(8,128)} %get-tuple-element.60), channel_id=1, source_target_pairs={{0,8},{1,9},{2,10},{3,11},{4,12},{5,13},{6,14},{7,15},{8,0},{9,1},... | collective-permute-start | bytes 8650760 | tf_op jit(solution)/shard_map/ppermute | solution.py:815
  399.6 3.2 copy-start.6
  404.5 256.0 %all-gather.13.cloned.1.call-start = ((), (), s32[]{:S(2)}) async-start(), calls=%async_computation.2 | async-start | bytes 4456448 | tf_op jit(solution)/shard_map/all_gather | solution.py:820
  404.8 142.8 %copy-start.8 = (f32[32,2048]{1,0:T(8,128)S(1)}, f32[32,2048]{1,0:T(8,128)}, u32[]{:S(2)}) copy-start(f32[32,2048]{1,0:T(8,128)} %get-tuple-element.69) | copy-start | bytes 786436
  404.8 144.3 %copy-start.3 = (f32[48,8,512]{2,1,0:T(8,128)S(1)}, f32[48,8,512]{2,1,0:T(8,128)}, u32[]{:S(2)}) copy-start(f32[48,8,512]{2,1,0:T(8,128)} %get-tuple-element.75) | copy-start | bytes 2359300
  404.8 157.5 %copy-start.4 = (f32[32,2048]{1,0:T(8,128)S(1)}, f32[32,2048]{1,0:T(8,128)}, u32[]{:S(2)}) copy-start(f32[32,2048]{1,0:T(8,128)} %get-tuple-element.66) | copy-start | bytes 786436
  404.8 9.3 %collective-permute-start.2 = (f32[2,512,1280]{2,1,0:T(8,128)}, f32[2,512,1280]{2,1,0:T(8,128)}, u32[]{:S(2)}, u32[]{:S(2)}) collective-permute-start(f32[2,512,1280]{2,1,0:T(8,128)} %get-tuple-element.64), channel_id=1, source_target_pairs={{0,1},{1,0},{2,3},{3,2},{4,5},{5,4},{6,7},{7,6},{8,9},{9,8},{10,11... | collective-permute-start | bytes 15728648 | tf_op jit(solution)/shard_map/ppermute | solution.py:821
  547.1 56.5 %collective-permute-start.4 = (f32[6,512,1280]{2,1,0:T(8,128)}, f32[6,512,1280]{2,1,0:T(8,128)}, u32[]{:S(2)}, u32[]{:S(2)}) collective-permute-start(f32[6,512,1280]{2,1,0:T(8,128)} %get-tuple-element.72), channel_id=1, source_target_pairs={{0,1},{1,0},{2,3},{3,2},{4,5},{5,4},{6,7},{7,6},{8,9},{9,8},{10,11... | collective-permute-start | bytes 47185928 | tf_op jit(solution)/shard_map/ppermute | solution.py:821
  547.5 47.1 %collective-permute-start.5 = (f32[4,512,1280]{2,1,0:T(8,128)}, f32[4,512,1280]{2,1,0:T(8,128)}, u32[]{:S(2)}, u32[]{:S(2)}) collective-permute-start(f32[4,512,1280]{2,1,0:T(8,128)} %get-tuple-element.73), channel_id=1, source_target_pairs={{0,1},{1,0},{2,3},{3,2},{4,5},{5,4},{6,7},{7,6},{8,9},{9,8},{10,11... | collective-permute-start | bytes 31457288 | tf_op jit(solution)/shard_map/ppermute | solution.py:821
  547.7 14.6 %collective-permute-start.3 = (f32[32,2048]{1,0:T(8,128)S(1)}, f32[32,2048]{1,0:T(8,128)S(1)}, u32[]{:S(2)}, u32[]{:S(2)}) collective-permute-start(f32[32,2048]{1,0:T(8,128)S(1)} %copy-done.8), channel_id=1, source_target_pairs={{0,8},{1,9},{2,10},{3,11},{4,12},{5,13},{6,14},{7,15},{8,0},{9,1},... | collective-permute-start | bytes 786440 | tf_op jit(solution)/shard_map/ppermute | solution.py:815
  615.7 5.9 copy-start
  629.7 30.8 %copy-start.5 = (f32[8,2048]{1,0:T(8,128)}, f32[8,2048]{1,0:T(8,128)S(1)}, u32[]{:S(2)}) copy-start(f32[8,2048]{1,0:T(8,128)S(1)} %bitcast_reduce_fusion) | copy-start | bytes 196612
  660.6 2.2 copy-start.1
  662.8 3.1 slice-start
Sparse Core Ops, SparseCore 0:
  92.9 42.9 all-gather.8
  139.3 47.0 all-gather.10
  319.0 88.3 all-gather.16
  409.5 185.1 all-gather.14
  596.8 35.6 all-gather.12

commit v3 on v2

--- a/solution.py
+++ b/solution.py
@@ -73,7 +73,7 @@
 
 
 def fwd_kernel(x_hbm, w_hbm, b_ref, gates_hbm, cp_hbm, hp_hbm, xs_hbm, xl_hbm,
-               w, xbuf, xout, gates, cprev, hprev, z0, z1, wsem, insem, recv, send, lastsem, osem):
+               w, xbuf, xout, gates, cprev, hprev, wsem, insem, recv, send, lastsem, osem):
     base, index, stage = place()
     first, last = stage == 0, stage == S - 1
     nxt = base + gray(lax.rem(stage + 1, S))
@@ -128,14 +128,7 @@
     lax.fori_loop(0, T // CH, lambda k, _: feed(k), 0)
     bias = b_ref[pl.ds(stage, 1), :]
 
-    def project(zref, t):
-        xt = rows_of(xbuf[t].astype(F32)).astype(BF16)
-        for n in range(0, G4, HB):
-            zref[:, n:n + HB] = dot(xt, w[0:H, n:n + HB]) + bias[:, n:n + HB]
-
     wcopy.wait()
-    arrived(jnp.int32(0))
-    project(z0, 0)
 
     kept = ((gates, gates_hbm), (cprev, cp_hbm), (hprev, hp_hbm), (xbuf, xs_hbm))
 
@@ -146,18 +139,16 @@
     def two(p, state):
         for u in range(2):
             t = 2 * p + u
-            zc, zn = ((z0, z1), (z1, z0))[u]
 
             @pl.when(t > 0)
             def _():
                 pass_on(t - 1)
                 save(t - 1)
 
-            @pl.when(t + 1 < T)
-            def _():
-                arrived(t + 1)
-
+            arrived(t)
             ha, hc, ca, cc = state
+            xt = rows_of(xbuf[t].astype(F32))
+            xlow = xt.astype(BF16)
             hlow = jnp.concatenate([ha, hc], axis=1).astype(BF16)
             hprev[t] = hlow
             cprev[t, :, 0:HB] = ca
@@ -167,15 +158,13 @@
                 zz = []
                 for g in range(4):
                     cols = slice(g * H + q * HB, g * H + q * HB + HB)
-                    zz.append(zc[:, cols] + dot(hlow, w[H:2 * H, cols]))
+                    zz.append(dot(xlow, w[0:H, cols]) + dot(hlow, w[H:2 * H, cols]) + bias[:, cols])
                 gi, gf, gg, go = jax.nn.sigmoid(zz[0]), jax.nn.sigmoid(zz[1]), jnp.tanh(zz[2]), jax.nn.sigmoid(zz[3])
                 cn = gf * (ca, cc)[q] + gi * gg
                 nh.append(go * jnp.tanh(cn))
                 nc.append(cn)
                 for g, val in enumerate((gi, gf, gg, go)):
                     gates[t, :, g * H + q * HB:g * H + q * HB + HB] = val
-            project(zn, jnp.minimum(t + 1, T - 1))
-            xt = rows_of(xbuf[t].astype(F32))
             xout[t] = groups_of(xt + jnp.concatenate(nh, axis=1)).astype(BF16)
             state = (nh[0], nh[1], nc[0], nc[1])
         return state
@@ -213,7 +202,7 @@
         out_specs=(HBM,) * 5,
         scratch_shapes=[pltpu.VMEM((2 * H, G4), BF16), pltpu.VMEM((T, S, R, H), BF16), pltpu.VMEM((T, S, R, H), BF16),
                         pltpu.VMEM((T, Q, G4), F32), pltpu.VMEM((T, Q, H), F32), pltpu.VMEM((T, Q, H), BF16)]
-        + [pltpu.VMEM((Q, G4), F32)] * 2 + [DMA((1,)), DMA, DMA((T,)), DMA, DMA, DMA((4,))],
+        + [DMA((1,)), DMA, DMA((T,)), DMA, DMA, DMA((4,))],
         compiler_params=pltpu.CompilerParams(vmem_limit_bytes=52 * MIB, collective_id=0, has_side_effects=True),
         cost_estimate=pl.CostEstimate(flops=60_000_000_000, bytes_accessed=80_000_000, transcendentals=0),
         name="lstm_fwd",
@@ -416,7 +405,7 @@
 RB = 64
 
 
-def head_kernel(x_ref, t_ref, w_hbm, dx_ref, lse_ref, lg, g0, g1, wv, mx, sm, tb, wsem):
+def head_kernel(x_ref, t_ref, w_hbm, dx_ref, stats_ref, lg, g0, g1, wv, mx, sm, tb, wsem):
     def wcopy(b):
         buf = lax.rem(b, NW)
         return pltpu.make_async_copy(w_hbm.at[:, pl.ds(pl.multiple_of(lax.rem(b, NVB) * VB, VB), VB)], wv.at[buf], wsem.at[buf])
@@ -465,9 +454,10 @@
         top = jnp.max(mx[rows, :], axis=1, keepdims=True)
         tot = jnp.sum(sm[rows, :] * jnp.exp(mx[rows, :] - top), axis=1, keepdims=True)
         lse = top + jnp.log(tot)
-        lse_ref[rows, :] = lse
         mx[rows, :] = jnp.broadcast_to(lse, (LANE, LANE))
         tb[rows, :] = jnp.broadcast_to(t_ref[rows, :], (LANE, LANE))
+        lane = lax.broadcasted_iota(jnp.int32, (LANE, LANE), 1)
+        stats_ref[rows, :] = jnp.where(lane < LANE // 2, mx[rows, :], tb[rows, :].astype(F32))
 
     for r in range(0, N, LANE):
         finish(r)
@@ -514,7 +504,7 @@
 def head(x, tgt, w_vocab):
     return pl.pallas_call(
         head_kernel,
-        out_shape=(jax.ShapeDtypeStruct((N, H), F32), jax.ShapeDtypeStruct((N, 1), F32)),
+        out_shape=(jax.ShapeDtypeStruct((N, H), F32), jax.ShapeDtypeStruct((N, LANE), F32)),
         in_specs=[VMEM, VMEM, ANY],
         out_specs=(VMEM, VMEM),
         scratch_shapes=[pltpu.VMEM((NVB, N, VB), F32), pltpu.VMEM((N, VB), BF16), pltpu.VMEM((N, VB), BF16), pltpu.VMEM((NW, H, VB), BF16),
@@ -798,9 +788,7 @@
         tgt = jnp.swapaxes(tgt_rows, 0, 1).reshape(N, 1)
         gates, cprev, hprev, xs, top = forward(jnp.swapaxes(x_rows, 0, 1), w_lstm, b_lstm)
         top = top.reshape(N, H)
-        d_top, lse = head(top, tgt, w_vocab)
-        half = (N, LANE // 2)
-        stats = jnp.concatenate([jnp.broadcast_to(lse, half), jnp.broadcast_to(tgt.astype(F32), half)], axis=1)
+        d_top, stats = head(top, tgt, w_vocab)
         x_all = lax.all_gather(top, 'data', axis=0, tiled=True)
         stats = lax.all_gather(stats, 'data', axis=0, tiled=True)
         d_top, x_all = lax.optimization_barrier((d_top, x_all))

time: 676 us -> 671 us (level)
  transfers between devices with their start and end apart: 11 -> 11, of which waited for: 3 -> 3; matrix products, arithmetic and copies ran while one was open for 2% -> 1% of each run, Pallas kernels for 73% -> 73%
where the time goes in v3:
time: 671 us; the launch traced here: 668 us
  Pallas kernels  573 us (85%)
  waiting for transfers between devices  52.8 us (8%)
  between operations  14.1 us (2%)
  local copies, waits for them, and re-layouts  12.4 us (2%)
  other arithmetic  11.7 us (2%)
    pallas_call x3, Pallas kernels, grad_vocab(): pl.pallas_call(functools.partial(dwv_kernel, lo, hi, counts), out_shape=o...  259 us
    pallas_call x1, Pallas kernels, backward(): pl.pallas_call(bwd_kernel, out_shape=tuple((jax.ShapeDtypeStruct((rows, G...  129 us
    pallas_call x1, Pallas kernels, forward(): pl.pallas_call(fwd_kernel, out_shape=(jax.ShapeDtypeStruct((T, Q, G4), F3...  80.8 us
    pallas_call x5, Pallas kernels, copy_call(): pl.pallas_call(kernel, out_shape=jax.ShapeDtypeStruct(out, F32), in_specs...  61.5 us
    pallas_call x1, Pallas kernels, head(): pl.pallas_call(head_kernel, out_shape=(jax.ShapeDtypeStruct((N, H), F32),...  43 us
    ppermute x3, waiting for transfers between devices, local_grads(): swapped.append((SPLITS[i], lax.ppermute(sent, 'data', other_core)))  40.8 us
  transfers between devices with their start and end apart: 11, of which 3 were waited for; matrix products, arithmetic and copies ran while one was open for 1% of the time, Pallas kernels for 73%

profile of v3, /device:TPU:0, one launch (start us, length us, event | category | flops | bytes accessed | tf_op | source)
XLA Modules:
  0.0 668.2 jit_solution(774467365566771623)
XLA Ops:
  7.2 0.0 all-gather.9.cloned.1.call-start
  7.2 1.2 copy.27
  8.4 0.0 copy-start.2
  8.4 0.8 copy-done.2
  9.3 80.8 %lstm_fwd.1 = (f32[48,64,2048]{2,1,0:T(8,128)}, f32[48,64,512]{2,1,0:T(8,128)}, bf16[48,64,512]{2,1,0:T(8,128)(2,1)}, bf16[48,8,8,512]{3,2,1,0:T(8,128)(2,1)}, bf16[48,8,512]{2,1,0:T(8,128)(2,1)}) custom-call(bf16[48,8,512]{2,1,0:T(8,128)(2,1)S(1)} %bitcast.14, bf16[8,1024,2048]{2,1,0:T(8,128)(2,1)} %w_hbm.8, f32[8,2048]{1,0:T(8,128)S(1)} %copy-done.2), custom_call_target="tpu_custom_call" | custom-call | flops 60000002048 | bytes 80000000 | tf_op jit(solution)/shard_map/lstm_fwd/pallas_call | solution.py:196
  90.1 0.0 all-gather.9.cloned.1.call-update
  90.1 0.0 all-gather.11.cloned.1.call-start
  90.1 0.1 copy.23
  90.2 0.8 reshape.25.t_ref
  91.0 43.0 %head.1 = (f32[384,512]{1,0:T(8,128)}, f32[384,128]{1,0:T(8,128)}) custom-call(bf16[384,512]{1,0:T(8,128)(2,1)} %bitcast.1.x_ref, s32[384,1]{1,0:T(8,128)} %reshape.25.t_ref, bf16[512,32000]{1,0:T(8,128)(2,1)} %w_hbm.11), custom_call_target="tpu_custom_call" | custom-call | flops 40000000000 | bytes 70000000 | tf_op jit(solution)/shard_map/head/pallas_call | solution.py:505
  134.1 0.0 all-gather.11.cloned.1.call-update
  134.1 0.0 all-gather.17.cloned.1.call-start
  134.1 0.0 all-gather.9.cloned.1.call-done.x_hbm
  134.2 128.7 %lstm_bwd.1 = (f32[256,2048]{1,0:T(8,128)}, f32[352,2048]{1,0:T(8,128)}, f32[32,2048]{1,0:T(8,128)}, f32[352,2048]{1,0:T(8,128)}, f32[32,2048]{1,0:T(8,128)}, /*index=5*/f32[8,2048]{1,0:T(8,128)}, f32[48,8,512]{2,1,0:T(8,128)}) custom-call(f32[48,8,512]{2,1,0:T(8,128)} %bitcast.19, f32[48,64,2048]{2,1,0:T(8,128)} %get-tuple-element.43.gates_hbm, ...), custom_call_target="tpu_custom_call" | custom-call | flops 109999996928 | bytes 80000000 | tf_op jit(solution)/shard_map/lstm_bwd/pallas_call | solution.py:385
  262.9 1.5 collective-permute-start
  264.4 45.6 %dwv.3 = (f32[512,32000]{1,0:T(8,128)}, f32[2,512,1280]{2,1,0:T(8,128)}) custom-call(bf16[6144,512]{1,0:T(8,128)(2,1)} %all-gather.9.cloned.1.call-done.x_hbm, f32[6144,128]{1,0:T(8,128)} %all-gather.11.cloned.1.call-done.st_ref, bf16[512,32000]{1,0:T(8,128)(2,1)} %w_hbm.11), custom_call_target="tpu_custom_call" | custom-call | flops 40000000000 | bytes 100000000 | tf_op jit(solution)/shard_map/dwv/pallas_call | solution.py:689
  310.0 3.9 add.9
  313.9 0.0 all-gather.17.cloned.1.call-update
  314.0 0.0 all-gather.15.cloned.1.call-start
  314.0 0.6 collective-permute-start.1
  314.6 80.0 %dwv.4 = (f32[512,32000]{1,0:T(8,128)}, f32[4,512,1280]{2,1,0:T(8,128)}) custom-call(bf16[6144,512]{1,0:T(8,128)(2,1)} %all-gather.9.cloned.1.call-done.x_hbm, f32[6144,128]{1,0:T(8,128)} %all-gather.11.cloned.1.call-done.st_ref, bf16[512,32000]{1,0:T(8,128)(2,1)} %w_hbm.11, f32[512,32000]{1,0:T(8,128)} %get-tuple-element.55.rest_0_), custom_call_target="tpu_custom_call", output_to_operand_aliasing={{0}: (3, {})} | custom-call | flops 80000000000 | bytes 100000000 | tf_op jit(solution)/shard_map/dwv/pallas_call | solution.py:689
  394.7 3.2 add.10
  397.8 1.8 pad_maximum_fusion
  399.6 0.0 all-gather.15.cloned.1.call-update
  399.6 0.3 all-gather.13.cloned.1.call-start
  399.9 0.0 collective-permute-start.2
  400.0 9.3 %collective-permute-done.2.rest_1_ = f32[2,512,1280]{2,1,0:T(8,128)} collective-permute-done((f32[2,512,1280]{2,1,0:T(8,128)}, f32[2,512,1280]{2,1,0:T(8,128)}, u32[]{:S(2)}, u32[]{:S(2)}) %collective-permute-start.2) | collective-permute-done | bytes 5242912 | tf_op jit(solution)/shard_map/ppermute | solution.py:809
  409.3 132.9 %dwv.5 = (f32[512,32000]{1,0:T(8,128)}, f32[6,512,1280]{2,1,0:T(8,128)}) custom-call(bf16[6144,512]{1,0:T(8,128)(2,1)} %all-gather.9.cloned.1.call-done.x_hbm, f32[6144,128]{1,0:T(8,128)} %all-gather.11.cloned.1.call-done.st_ref, bf16[512,32000]{1,0:T(8,128)(2,1)} %w_hbm.11, ...), custom_call_target="tpu_custom_call", output_to_operand_aliasing={{0}: (3, {})} | custom-call | flops 140000002048 | bytes 100000000 | tf_op jit(solution)/shard_map/dwv/pallas_call | solution.py:689
  542.2 0.4 collective-permute-start.4
  542.6 0.1 collective-permute-start.5
  542.7 1.4 collective-permute-start.3
  544.2 1.3 copy.25
  545.5 11.9 %collective-permute-done.3 = f32[32,2048]{1,0:T(8,128)S(1)} collective-permute-done((f32[32,2048]{1,0:T(8,128)S(1)}, f32[32,2048]{1,0:T(8,128)S(1)}, u32[]{:S(2)}, u32[]{:S(2)}) %collective-permute-start.3) | collective-permute-done | bytes 262176 | tf_op jit(solution)/shard_map/ppermute | solution.py:803
  557.4 0.7 add.11
  558.1 0.0 all-gather.13.cloned.1.call-update
  558.2 31.5 %collective-permute-done.5.src = f32[4,512,1280]{2,1,0:T(8,128)} collective-permute-done((f32[4,512,1280]{2,1,0:T(8,128)}, f32[4,512,1280]{2,1,0:T(8,128)}, u32[]{:S(2)}, u32[]{:S(2)}) %collective-permute-start.5) | collective-permute-done | bytes 10485792 | tf_op jit(solution)/shard_map/ppermute | solution.py:809
  589.7 9.0 %shard_map.87._ = f32[512,32000]{1,0:T(8,128)} custom-call(f32[4,512,1280]{2,1,0:T(8,128)} %collective-permute-done.5.src, f32[512,32000]{1,0:T(8,128)} %get-tuple-element.74._), custom_call_target="tpu_custom_call", output_to_operand_aliasing={{}: (1, {})} | custom-call | flops 20000000000 | bytes 130000000 | tf_op jit(solution)/shard_map/pallas_call | solution.py:740
  598.7 12.1 %shard_map.88 = f32[512,32000]{1,0:T(8,128)} custom-call(f32[6,512,1280]{2,1,0:T(8,128)} %collective-permute-done.4.src, f32[512,32000]{1,0:T(8,128)} %shard_map.87._), custom_call_target="tpu_custom_call", output_to_operand_aliasing={{}: (1, {})} | custom-call | flops 20000000000 | bytes 130000000 | tf_op jit(solution)/shard_map/pallas_call | solution.py:740
  610.8 0.0 all-gather.17.cloned.1.call-done
  610.8 5.9 copy-done
  616.7 6.6 shard_map.84.rest_0_
  623.3 0.0 all-gather.15.cloned.1.call-done
  623.3 1.5 slice_reduce_fusion
  624.9 30.8 %shard_map.85.rest_0_ = f32[8,1024,2048]{2,1,0:T(8,128)} custom-call(f32[16,360,2048]{2,1,0:T(8,128)} %bitcast.16, f32[8,1024,2048]{2,1,0:T(8,128)} %shard_map.84.rest_0_), custom_call_target="tpu_custom_call", output_to_operand_aliasing={{}: (1, {})} | custom-call | flops 20000000000 | bytes 130000000 | tf_op jit(solution)/shard_map/pallas_call | solution.py:740
  655.7 0.0 all-gather.13.cloned.1.call-done
  655.7 2.2 copy-done.1
  657.9 3.1 shard_map.86
  661.0 0.7 pad_maximum_fusion.1
  (22 shorter events, 0.1 us)
Async XLA Ops:
  7.2 127.0 %all-gather.9.cloned.1.call-start = ((), (), s32[]{:S(2)}) async-start(), calls=%async_computation | async-start | bytes 6684672 | tf_op jit(solution)/shard_map/all_gather | solution.py:792
  8.4 0.8 copy-start.2
  9.3 80.9 %copy-start.7 = (s32[8,48]{1,0:T(8,128)S(1)}, s32[8,48]{1,0:T(8,128)}, u32[]{:S(2)}) copy-start(s32[8,48]{1,0:T(8,128)} %param.6) | copy-start | bytes 4612
  90.1 174.3 %all-gather.11.cloned.1.call-start = ((), (), s32[]{:S(2)}) async-start(), calls=%async_computation.1 | async-start | bytes 3342336 | tf_op jit(solution)/shard_map/all_gather | solution.py:793
  134.1 476.7 %all-gather.17.cloned.1.call-start = ((), (), s32[]{:S(2)}) async-start(), calls=%async_computation.4 | async-start | bytes 18874368 | tf_op jit(solution)/shard_map/all_gather | solution.py:808
  262.9 47.1 %collective-permute-start = (f32[256,2048]{1,0:T(8,128)}, f32[256,2048]{1,0:T(8,128)}, u32[]{:S(2)}, u32[]{:S(2)}) collective-permute-start(f32[256,2048]{1,0:T(8,128)} %get-tuple-element.53), channel_id=1, source_target_pairs={{0,8},{1,9},{2,10},{3,11},{4,12},{5,13},{6,14},{7,15},{8,0},{9,1},... | collective-permute-start | bytes 6291464 | tf_op jit(solution)/shard_map/ppermute | solution.py:803
  314.0 309.4 %all-gather.15.cloned.1.call-start = ((), (), s32[]{:S(2)}) async-start(), calls=%async_computation.3 | async-start | bytes 50135040 | tf_op jit(solution)/shard_map/all_gather | solution.py:808
  314.0 80.6 %collective-permute-start.1 = (f32[352,2048]{1,0:T(8,128)}, f32[352,2048]{1,0:T(8,128)}, u32[]{:S(2)}, u32[]{:S(2)}) collective-permute-start(f32[352,2048]{1,0:T(8,128)} %get-tuple-element.60), channel_id=1, source_target_pairs={{0,8},{1,9},{2,10},{3,11},{4,12},{5,13},{6,14},{7,15},{8,0},{9,1},... | collective-permute-start | bytes 8650760 | tf_op jit(solution)/shard_map/ppermute | solution.py:803
  394.6 3.2 copy-start.6
  399.6 256.0 %all-gather.13.cloned.1.call-start = ((), (), s32[]{:S(2)}) async-start(), calls=%async_computation.2 | async-start | bytes 4456448 | tf_op jit(solution)/shard_map/all_gather | solution.py:808
  399.9 142.8 %copy-start.8 = (f32[32,2048]{1,0:T(8,128)S(1)}, f32[32,2048]{1,0:T(8,128)}, u32[]{:S(2)}) copy-start(f32[32,2048]{1,0:T(8,128)} %get-tuple-element.69) | copy-start | bytes 786436
  399.9 144.3 %copy-start.3 = (f32[48,8,512]{2,1,0:T(8,128)S(1)}, f32[48,8,512]{2,1,0:T(8,128)}, u32[]{:S(2)}) copy-start(f32[48,8,512]{2,1,0:T(8,128)} %get-tuple-element.75) | copy-start | bytes 2359300
  399.9 157.5 %copy-start.4 = (f32[32,2048]{1,0:T(8,128)S(1)}, f32[32,2048]{1,0:T(8,128)}, u32[]{:S(2)}) copy-start(f32[32,2048]{1,0:T(8,128)} %get-tuple-element.66) | copy-start | bytes 786436
  399.9 9.3 %collective-permute-start.2 = (f32[2,512,1280]{2,1,0:T(8,128)}, f32[2,512,1280]{2,1,0:T(8,128)}, u32[]{:S(2)}, u32[]{:S(2)}) collective-permute-start(f32[2,512,1280]{2,1,0:T(8,128)} %get-tuple-element.64), channel_id=1, source_target_pairs={{0,1},{1,0},{2,3},{3,2},{4,5},{5,4},{6,7},{7,6},{8,9},{9,8},{10,11... | collective-permute-start | bytes 15728648 | tf_op jit(solution)/shard_map/ppermute | solution.py:809
  542.2 56.5 %collective-permute-start.4 = (f32[6,512,1280]{2,1,0:T(8,128)}, f32[6,512,1280]{2,1,0:T(8,128)}, u32[]{:S(2)}, u32[]{:S(2)}) collective-permute-start(f32[6,512,1280]{2,1,0:T(8,128)} %get-tuple-element.72), channel_id=1, source_target_pairs={{0,1},{1,0},{2,3},{3,2},{4,5},{5,4},{6,7},{7,6},{8,9},{9,8},{10,11... | collective-permute-start | bytes 47185928 | tf_op jit(solution)/shard_map/ppermute | solution.py:809
  542.6 47.0 %collective-permute-start.5 = (f32[4,512,1280]{2,1,0:T(8,128)}, f32[4,512,1280]{2,1,0:T(8,128)}, u32[]{:S(2)}, u32[]{:S(2)}) collective-permute-start(f32[4,512,1280]{2,1,0:T(8,128)} %get-tuple-element.73), channel_id=1, source_target_pairs={{0,1},{1,0},{2,3},{3,2},{4,5},{5,4},{6,7},{7,6},{8,9},{9,8},{10,11... | collective-permute-start | bytes 31457288 | tf_op jit(solution)/shard_map/ppermute | solution.py:809
  542.7 14.6 %collective-permute-start.3 = (f32[32,2048]{1,0:T(8,128)S(1)}, f32[32,2048]{1,0:T(8,128)S(1)}, u32[]{:S(2)}, u32[]{:S(2)}) collective-permute-start(f32[32,2048]{1,0:T(8,128)S(1)} %copy-done.8), channel_id=1, source_target_pairs={{0,8},{1,9},{2,10},{3,11},{4,12},{5,13},{6,14},{7,15},{8,0},{9,1},... | collective-permute-start | bytes 786440 | tf_op jit(solution)/shard_map/ppermute | solution.py:803
  610.8 5.9 copy-start
  624.8 30.8 %copy-start.5 = (f32[8,2048]{1,0:T(8,128)}, f32[8,2048]{1,0:T(8,128)S(1)}, u32[]{:S(2)}) copy-start(f32[8,2048]{1,0:T(8,128)S(1)} %bitcast_reduce_fusion) | copy-start | bytes 196612
  655.7 2.2 copy-start.1
  657.9 3.1 slice-start
Sparse Core Ops, SparseCore 0:
  90.2 42.9 all-gather.8
  136.0 45.4 all-gather.10
  314.1 88.3 all-gather.16
  404.6 185.1 all-gather.14
  591.9 35.6 all-gather.12

commit v4 on v3

--- a/solution.py
+++ b/solution.py
@@ -18,6 +18,7 @@
 V = 32000
 LANE = 128
 NDEV = 16
+CO = 2
 CH = 4
 NR = 6
 PIECES = ((0, 0, 256), (256, 384, 352), (608, 384, 32))
@@ -83,15 +84,15 @@
     plane_wait()
 
     def feed(k):
-        ts = pl.ds(k * CH, CH)
+        ts = pl.ds(k * CO, CO)
 
         @pl.when(first)
         def _():
-            pltpu.make_async_copy(x_hbm.at[ts], xbuf.at[ts, 0], recv.at[k * CH]).start()
+            pltpu.make_async_copy(x_hbm.at[ts], xbuf.at[ts, 0], recv.at[k * CO]).start()
 
         @pl.when(jnp.logical_not(first))
         def _():
-            pltpu.make_async_remote_copy(x_hbm.at[ts], xbuf.at[ts, index], insem, recv.at[k * CH],
+            pltpu.make_async_remote_copy(x_hbm.at[ts], xbuf.at[ts, index], insem, recv.at[k * CO],
                                          device_id=(base,), device_id_type=MESH).start()
 
         return 0
@@ -100,7 +101,7 @@
         return pltpu.make_async_remote_copy(xout.at[t], xbuf.at[t], send, recv.at[t], device_id=(nxt,), device_id_type=MESH)
 
     def final_out(t, i):
-        ts = pl.ds(t, CH)
+        ts = pl.ds(t, CO)
         if i == LAST:
             return pltpu.make_async_copy(xout.at[ts, i], xl_hbm.at[ts], lastsem)
         return pltpu.make_async_remote_copy(xout.at[ts, i], xl_hbm.at[ts], send, lastsem, device_id=(base + i,), device_id_type=MESH)
@@ -110,9 +111,9 @@
         def _():
             step_out(t).wait_recv()
 
-        @pl.when(first & (lax.rem(t, CH) == 0))
-        def _():
-            ts = pl.ds(t, CH)
+        @pl.when(first & (lax.rem(t, CO) == 0))
+        def _():
+            ts = pl.ds(t, CO)
             pltpu.make_async_remote_copy(xout.at[ts], xbuf.at[ts], send, recv.at[t], device_id=(nxt,), device_id_type=MESH).wait_recv()
 
     def pass_on(t):
@@ -120,12 +121,12 @@
         def _():
             step_out(t).start()
 
-        @pl.when(last & (lax.rem(t, CH) == CH - 1))
+        @pl.when(last & (lax.rem(t, CO) == CO - 1))
         def _():
             for i in range(S):
-                final_out(t - CH + 1, i).start()
-
-    lax.fori_loop(0, T // CH, lambda k, _: feed(k), 0)
+                final_out(t - CO + 1, i).start()
+
+    lax.fori_loop(0, T // CO, lambda k, _: feed(k), 0)
     bias = b_ref[pl.ds(stage, 1), :]
 
     wcopy.wait()
@@ -222,8 +223,8 @@
     wcopy.start()
 
     def feed(k):
-        t = T - CH - k * CH
-        ts = pl.ds(t, CH)
+        t = T - CO - k * CO
+        ts = pl.ds(t, CO)
 
         @pl.when(last)
         def _():
@@ -240,7 +241,7 @@
         return pltpu.make_async_remote_copy(dout.at[t], dbuf.at[t], send, recv.at[t], device_id=(prv,), device_id_type=MESH)
 
     def final_out(t, i):
-        ts = pl.ds(t, CH)
+        ts = pl.ds(t, CO)
         if i == 0:
             return pltpu.make_async_copy(dout.at[ts, i], dx_hbm.at[ts], lastsem)
         return pltpu.make_async_remote_copy(dout.at[ts, i], dx_hbm.at[ts], send, lastsem, device_id=(base + i,), device_id_type=MESH)
@@ -250,17 +251,17 @@
         def _():
             step_out(t).wait_recv()
 
-        @pl.when(last & (lax.rem(t, CH) == CH - 1))
-        def _():
-            ts = pl.ds(t - CH + 1, CH)
-            pltpu.make_async_remote_copy(dout.at[ts], dbuf.at[ts], send, recv.at[t - CH + 1], device_id=(prv,), device_id_type=MESH).wait_recv()
+        @pl.when(last & (lax.rem(t, CO) == CO - 1))
+        def _():
+            ts = pl.ds(t - CO + 1, CO)
+            pltpu.make_async_remote_copy(dout.at[ts], dbuf.at[ts], send, recv.at[t - CO + 1], device_id=(prv,), device_id_type=MESH).wait_recv()
 
     def pass_on(t):
         @pl.when(jnp.logical_not(first))
         def _():
             step_out(t).start()
 
-        @pl.when(first & (lax.rem(t, CH) == 0))
+        @pl.when(first & (lax.rem(t, CO) == 0))
         def _():
             for i in range(S):
                 final_out(t, i).start()
@@ -274,7 +275,7 @@
         for cp in loads(t):
             cp.start()
     plane_wait()
-    lax.fori_loop(0, T // CH, lambda k, _: feed(k), 0)
+    lax.fori_loop(0, T // CO, lambda k, _: feed(k), 0)
     db_ref[...] = jnp.zeros(db_ref.shape, F32)
     acc[...] = jnp.zeros(acc.shape, F32)
     wcopy.wait()
@@ -286,9 +287,10 @@
 
     lax.fori_loop(0, G4 // HB, turn, 0)
 
-    def weight():
-        for n in range(0, G4, HB):
-            acc[:, n:n + HB] += dot(ut[...], dall[:, n:n + HB])
+    def weight(buf, part):
+        for n in range(0, G4 // CH, HB):
+            cols = pl.ds(pl.multiple_of(part * (G4 // CH) + n, HB), HB)
+            acc[:, cols] += dot(ut[buf], dall[buf, :, cols])
 
     def two(n, state):
         p = T // 2 - 1 - n
@@ -303,10 +305,11 @@
             def _():
                 pass_on(t + 1)
 
-            if u == 1:
-                @pl.when((p < T // 2 - 1) & (lax.rem(p, CH // 2) == CH // 2 - 1))
-                def _():
-                    weight()
+            buf = lax.rem(t // CH, 2)
+
+            @pl.when(t < T - CH)
+            def _():
+                weight(1 - buf, lax.rem(t, CH))
 
             arrived(t)
             ea, ec, da, dc_ = state
@@ -330,7 +333,7 @@
             for i, v in enumerate(v for ps in parts for v in ps):
                 cols = slice(i * HB, i * HB + HB)
                 low = v.astype(BF16)
-                dall[trows, cols] = low
+                dall[buf, trows, cols] = low
                 lows.append(low)
                 db_ref[:, cols] += jnp.sum(v.reshape(Q // R, R, HB), axis=0)
             lowz = jnp.concatenate(lows, axis=1)
@@ -348,7 +351,7 @@
 
         tcols = pl.ds(pl.multiple_of(lax.rem(p, CH // 2) * 2 * Q, 2 * Q), 2 * Q)
         for j in range(2):
-            ut[j * H:j * H + H, tcols] = jnp.concatenate([us[1][j], us[0][j]], axis=0).T.astype(BF16)
+            ut[buf, j * H:j * H + H, tcols] = jnp.concatenate([us[1][j], us[0][j]], axis=0).T.astype(BF16)
 
         return state
 
@@ -356,7 +359,7 @@
     lax.fori_loop(0, T // 2, two, (zero,) * 4)
     pass_on(jnp.int32(0))
 
-    weight()
+    lax.fori_loop(0, CH, lambda k, _: (weight(0, k), 0)[1], 0)
     outs = []
     for i, (dst, (row, step, rows), at) in enumerate(((both, PIECES[0], 0), (give1, PIECES[1], 1 - plane), (give2, PIECES[2], 1 - plane),
                                                       (own1, PIECES[1], plane), (own2, PIECES[2], plane))):
@@ -388,7 +391,7 @@
         in_specs=[ANY] * 6,
         out_specs=(HBM,) * 5 + (VMEM, HBM),
         scratch_shapes=[pltpu.VMEM((2 * H, G4), BF16), pltpu.VMEM((G4, 2 * H), BF16), pltpu.VMEM((T, S, R, H), F32),
-                        pltpu.VMEM((T, S, R, H), F32), pltpu.VMEM((CH * Q, G4), BF16), pltpu.VMEM((2 * H, CH * Q), BF16), pltpu.VMEM((2 * H, G4), F32)]
+                        pltpu.VMEM((T, S, R, H), F32), pltpu.VMEM((2, CH * Q, G4), BF16), pltpu.VMEM((2, 2 * H, CH * Q), BF16), pltpu.VMEM((2 * H, G4), F32)]
         + [pltpu.VMEM((NR, Q, G4), F32), pltpu.VMEM((NR, Q, H), F32), pltpu.VMEM((NR, Q, H), BF16), pltpu.VMEM((NR, S, R, H), BF16)]
         + [DMA((1,)), DMA, DMA((T,)), DMA, DMA, DMA((NR, 4)), DMA((5,))],
         compiler_params=pltpu.CompilerParams(vmem_limit_bytes=56 * MIB, collective_id=1, has_side_effects=True),

time: 671 us -> 677 us (level)
  Pallas kernels: 573 us -> 580 us
    pallas_call x1, Pallas kernels: 129 us -> 136 us  [backward(): pl.pallas_call(bwd_kernel, out_shape=tuple((jax.ShapeDtypeStruct((rows, G...]
where the time goes in v4:
time: 677 us; the launch traced here: 675 us
  Pallas kernels  580 us (86%)
  waiting for transfers between devices  52.7 us (8%)
  between operations  14.1 us (2%)
  local copies, waits for them, and re-layouts  12.9 us (2%)
  other arithmetic  11.7 us (2%)
    pallas_call x3, Pallas kernels, grad_vocab(): pl.pallas_call(functools.partial(dwv_kernel, lo, hi, counts), out_shape=o...  258 us
    pallas_call x1, Pallas kernels, backward(): pl.pallas_call(bwd_kernel, out_shape=tuple((jax.ShapeDtypeStruct((rows, G...  136 us
    pallas_call x1, Pallas kernels, forward(): pl.pallas_call(fwd_kernel, out_shape=(jax.ShapeDtypeStruct((T, Q, G4), F3...  80.8 us
    pallas_call x5, Pallas kernels, copy_call(): pl.pallas_call(kernel, out_shape=jax.ShapeDtypeStruct(out, F32), in_specs...  61.8 us
    pallas_call x1, Pallas kernels, head(): pl.pallas_call(head_kernel, out_shape=(jax.ShapeDtypeStruct((N, H), F32),...  43.2 us
    ppermute x3, waiting for transfers between devices, local_grads(): swapped.append((SPLITS[i], lax.ppermute(sent, 'data', other_core)))  39.9 us
  transfers between devices with their start and end apart: 11, of which 3 were waited for; matrix products, arithmetic and copies ran while one was open for 1% of the time, Pallas kernels for 73%

profile of v4, /device:TPU:0, one launch (start us, length us, event | category | flops | bytes accessed | tf_op | source)
XLA Modules:
  0.0 675.1 jit_solution(14605705931548593673)
XLA Ops:
  7.2 0.0 all-gather.9.cloned.1.call-start
  7.2 1.2 copy.27
  8.4 0.0 copy-start.2
  8.4 0.8 copy-done.2
  9.3 80.8 %lstm_fwd.1 = (f32[48,64,2048]{2,1,0:T(8,128)}, f32[48,64,512]{2,1,0:T(8,128)}, bf16[48,64,512]{2,1,0:T(8,128)(2,1)}, bf16[48,8,8,512]{3,2,1,0:T(8,128)(2,1)}, bf16[48,8,512]{2,1,0:T(8,128)(2,1)}) custom-call(bf16[48,8,512]{2,1,0:T(8,128)(2,1)S(1)} %bitcast.14, bf16[8,1024,2048]{2,1,0:T(8,128)(2,1)} %w_hbm.8, f32[8,2048]{1,0:T(8,128)S(1)} %copy-done.2), custom_call_target="tpu_custom_call" | custom-call | flops 60000002048 | bytes 80000000 | tf_op jit(solution)/shard_map/lstm_fwd/pallas_call | solution.py:197
  90.1 0.0 all-gather.9.cloned.1.call-update
  90.2 0.0 all-gather.11.cloned.1.call-start
  90.2 0.1 copy.23
  90.3 0.8 reshape.25.t_ref
  91.1 43.2 %head.1 = (f32[384,512]{1,0:T(8,128)}, f32[384,128]{1,0:T(8,128)}) custom-call(bf16[384,512]{1,0:T(8,128)(2,1)} %bitcast.1.x_ref, s32[384,1]{1,0:T(8,128)} %reshape.25.t_ref, bf16[512,32000]{1,0:T(8,128)(2,1)} %w_hbm.11), custom_call_target="tpu_custom_call" | custom-call | flops 40000000000 | bytes 70000000 | tf_op jit(solution)/shard_map/head/pallas_call | solution.py:508
  134.3 0.0 all-gather.11.cloned.1.call-update
  134.3 0.0 all-gather.17.cloned.1.call-start
  134.4 0.0 all-gather.9.cloned.1.call-done.x_hbm
  134.4 135.8 %lstm_bwd.1 = (f32[256,2048]{1,0:T(8,128)}, f32[352,2048]{1,0:T(8,128)}, f32[32,2048]{1,0:T(8,128)}, f32[352,2048]{1,0:T(8,128)}, f32[32,2048]{1,0:T(8,128)}, /*index=5*/f32[8,2048]{1,0:T(8,128)}, f32[48,8,512]{2,1,0:T(8,128)}) custom-call(f32[48,8,512]{2,1,0:T(8,128)} %bitcast.19, f32[48,64,2048]{2,1,0:T(8,128)} %get-tuple-element.43.gates_hbm, ...), custom_call_target="tpu_custom_call" | custom-call | flops 109999996928 | bytes 80000000 | tf_op jit(solution)/shard_map/lstm_bwd/pallas_call | solution.py:388
  270.3 0.8 collective-permute-start
  271.1 45.6 %dwv.3 = (f32[512,32000]{1,0:T(8,128)}, f32[2,512,1280]{2,1,0:T(8,128)}) custom-call(bf16[6144,512]{1,0:T(8,128)(2,1)} %all-gather.9.cloned.1.call-done.x_hbm, f32[6144,128]{1,0:T(8,128)} %all-gather.11.cloned.1.call-done.st_ref, bf16[512,32000]{1,0:T(8,128)(2,1)} %w_hbm.11), custom_call_target="tpu_custom_call" | custom-call | flops 40000000000 | bytes 100000000 | tf_op jit(solution)/shard_map/dwv/pallas_call | solution.py:692
  316.7 3.9 add.9
  320.6 0.0 all-gather.17.cloned.1.call-update
  320.7 0.0 all-gather.15.cloned.1.call-start
  320.7 1.2 collective-permute-start.1
  322.0 80.1 %dwv.4 = (f32[512,32000]{1,0:T(8,128)}, f32[4,512,1280]{2,1,0:T(8,128)}) custom-call(bf16[6144,512]{1,0:T(8,128)(2,1)} %all-gather.9.cloned.1.call-done.x_hbm, f32[6144,128]{1,0:T(8,128)} %all-gather.11.cloned.1.call-done.st_ref, bf16[512,32000]{1,0:T(8,128)(2,1)} %w_hbm.11, f32[512,32000]{1,0:T(8,128)} %get-tuple-element.55.rest_0_), custom_call_target="tpu_custom_call", output_to_operand_aliasing={{0}: (3, {})} | custom-call | flops 80000000000 | bytes 100000000 | tf_op jit(solution)/shard_map/dwv/pallas_call | solution.py:692
  402.1 3.1 add.10
  405.3 1.8 pad_maximum_fusion
  407.0 0.0 all-gather.15.cloned.1.call-update
  407.1 0.3 all-gather.13.cloned.1.call-start
  407.4 0.0 collective-permute-start.2
  407.4 9.0 %collective-permute-done.2.rest_1_ = f32[2,512,1280]{2,1,0:T(8,128)} collective-permute-done((f32[2,512,1280]{2,1,0:T(8,128)}, f32[2,512,1280]{2,1,0:T(8,128)}, u32[]{:S(2)}, u32[]{:S(2)}) %collective-permute-start.2) | collective-permute-done | bytes 5242912 | tf_op jit(solution)/shard_map/ppermute | solution.py:812
  416.4 132.6 %dwv.5 = (f32[512,32000]{1,0:T(8,128)}, f32[6,512,1280]{2,1,0:T(8,128)}) custom-call(bf16[6144,512]{1,0:T(8,128)(2,1)} %all-gather.9.cloned.1.call-done.x_hbm, f32[6144,128]{1,0:T(8,128)} %all-gather.11.cloned.1.call-done.st_ref, bf16[512,32000]{1,0:T(8,128)(2,1)} %w_hbm.11, ...), custom_call_target="tpu_custom_call", output_to_operand_aliasing={{0}: (3, {})} | custom-call | flops 140000002048 | bytes 100000000 | tf_op jit(solution)/shard_map/dwv/pallas_call | solution.py:692
  549.0 0.2 collective-permute-start.4
  549.3 0.3 collective-permute-start.5
  549.6 0.6 collective-permute-start.3
  550.2 1.3 copy.25
  551.5 12.6 %collective-permute-done.3 = f32[32,2048]{1,0:T(8,128)S(1)} collective-permute-done((f32[32,2048]{1,0:T(8,128)S(1)}, f32[32,2048]{1,0:T(8,128)S(1)}, u32[]{:S(2)}, u32[]{:S(2)}) %collective-permute-start.3) | collective-permute-done | bytes 262176 | tf_op jit(solution)/shard_map/ppermute | solution.py:806
  564.2 0.7 add.11
  564.9 0.0 all-gather.13.cloned.1.call-update
  564.9 30.9 %collective-permute-done.5.src = f32[4,512,1280]{2,1,0:T(8,128)} collective-permute-done((f32[4,512,1280]{2,1,0:T(8,128)}, f32[4,512,1280]{2,1,0:T(8,128)}, u32[]{:S(2)}, u32[]{:S(2)}) %collective-permute-start.5) | collective-permute-done | bytes 10485792 | tf_op jit(solution)/shard_map/ppermute | solution.py:812
  595.8 9.1 %shard_map.87._ = f32[512,32000]{1,0:T(8,128)} custom-call(f32[4,512,1280]{2,1,0:T(8,128)} %collective-permute-done.5.src, f32[512,32000]{1,0:T(8,128)} %get-tuple-element.74._), custom_call_target="tpu_custom_call", output_to_operand_aliasing={{}: (1, {})} | custom-call | flops 20000000000 | bytes 130000000 | tf_op jit(solution)/shard_map/pallas_call | solution.py:743
  604.9 12.1 %shard_map.88 = f32[512,32000]{1,0:T(8,128)} custom-call(f32[6,512,1280]{2,1,0:T(8,128)} %collective-permute-done.4.src, f32[512,32000]{1,0:T(8,128)} %shard_map.87._), custom_call_target="tpu_custom_call", output_to_operand_aliasing={{}: (1, {})} | custom-call | flops 20000000000 | bytes 130000000 | tf_op jit(solution)/shard_map/pallas_call | solution.py:743
  617.0 0.0 all-gather.17.cloned.1.call-done
  617.1 6.5 copy-done
  623.5 6.6 shard_map.84.rest_0_
  630.1 0.0 all-gather.15.cloned.1.call-done
  630.1 1.5 slice_reduce_fusion
  631.7 30.9 %shard_map.85.rest_0_ = f32[8,1024,2048]{2,1,0:T(8,128)} custom-call(f32[16,360,2048]{2,1,0:T(8,128)} %bitcast.16, f32[8,1024,2048]{2,1,0:T(8,128)} %shard_map.84.rest_0_), custom_call_target="tpu_custom_call", output_to_operand_aliasing={{}: (1, {})} | custom-call | flops 20000000000 | bytes 130000000 | tf_op jit(solution)/shard_map/pallas_call | solution.py:743
  662.6 0.0 all-gather.13.cloned.1.call-done
  662.6 2.2 copy-done.1
  664.8 3.1 shard_map.86
  667.9 0.7 pad_maximum_fusion.1
  (22 shorter events, 0.1 us)
Async XLA Ops:
  7.2 127.2 %all-gather.9.cloned.1.call-start = ((), (), s32[]{:S(2)}) async-start(), calls=%async_computation | async-start | bytes 6684672 | tf_op jit(solution)/shard_map/all_gather | solution.py:795
  8.4 0.8 copy-start.2
  9.3 80.9 %copy-start.7 = (s32[8,48]{1,0:T(8,128)S(1)}, s32[8,48]{1,0:T(8,128)}, u32[]{:S(2)}) copy-start(s32[8,48]{1,0:T(8,128)} %param.6) | copy-start | bytes 4612
  90.2 181.0 %all-gather.11.cloned.1.call-start = ((), (), s32[]{:S(2)}) async-start(), calls=%async_computation.1 | async-start | bytes 3342336 | tf_op jit(solution)/shard_map/all_gather | solution.py:796
  134.3 482.7 %all-gather.17.cloned.1.call-start = ((), (), s32[]{:S(2)}) async-start(), calls=%async_computation.4 | async-start | bytes 18874368 | tf_op jit(solution)/shard_map/all_gather | solution.py:811
  270.3 46.5 %collective-permute-start = (f32[256,2048]{1,0:T(8,128)}, f32[256,2048]{1,0:T(8,128)}, u32[]{:S(2)}, u32[]{:S(2)}) collective-permute-start(f32[256,2048]{1,0:T(8,128)} %get-tuple-element.53), channel_id=1, source_target_pairs={{0,8},{1,9},{2,10},{3,11},{4,12},{5,13},{6,14},{7,15},{8,0},{9,1},... | collective-permute-start | bytes 6291464 | tf_op jit(solution)/shard_map/ppermute | solution.py:806
  320.7 309.4 %all-gather.15.cloned.1.call-start = ((), (), s32[]{:S(2)}) async-start(), calls=%async_computation.3 | async-start | bytes 50135040 | tf_op jit(solution)/shard_map/all_gather | solution.py:811
  320.7 81.4 %collective-permute-start.1 = (f32[352,2048]{1,0:T(8,128)}, f32[352,2048]{1,0:T(8,128)}, u32[]{:S(2)}, u32[]{:S(2)}) collective-permute-start(f32[352,2048]{1,0:T(8,128)} %get-tuple-element.60), channel_id=1, source_target_pairs={{0,8},{1,9},{2,10},{3,11},{4,12},{5,13},{6,14},{7,15},{8,0},{9,1},... | collective-permute-start | bytes 8650760 | tf_op jit(solution)/shard_map/ppermute | solution.py:806
  402.1 3.2 copy-start.6
  407.1 255.5 %all-gather.13.cloned.1.call-start = ((), (), s32[]{:S(2)}) async-start(), calls=%async_computation.2 | async-start | bytes 4456448 | tf_op jit(solution)/shard_map/all_gather | solution.py:811
  407.3 142.2 %copy-start.8 = (f32[32,2048]{1,0:T(8,128)S(1)}, f32[32,2048]{1,0:T(8,128)}, u32[]{:S(2)}) copy-start(f32[32,2048]{1,0:T(8,128)} %get-tuple-element.69) | copy-start | bytes 786436
  407.4 142.8 %copy-start.3 = (f32[48,8,512]{2,1,0:T(8,128)S(1)}, f32[48,8,512]{2,1,0:T(8,128)}, u32[]{:S(2)}) copy-start(f32[48,8,512]{2,1,0:T(8,128)} %get-tuple-element.75) | copy-start | bytes 2359300
  407.4 156.8 %copy-start.4 = (f32[32,2048]{1,0:T(8,128)S(1)}, f32[32,2048]{1,0:T(8,128)}, u32[]{:S(2)}) copy-start(f32[32,2048]{1,0:T(8,128)} %get-tuple-element.66) | copy-start | bytes 786436
  407.4 9.0 %collective-permute-start.2 = (f32[2,512,1280]{2,1,0:T(8,128)}, f32[2,512,1280]{2,1,0:T(8,128)}, u32[]{:S(2)}, u32[]{:S(2)}) collective-permute-start(f32[2,512,1280]{2,1,0:T(8,128)} %get-tuple-element.64), channel_id=1, source_target_pairs={{0,1},{1,0},{2,3},{3,2},{4,5},{5,4},{6,7},{7,6},{8,9},{9,8},{10,11... | collective-permute-start | bytes 15728648 | tf_op jit(solution)/shard_map/ppermute | solution.py:812
  549.0 55.9 %collective-permute-start.4 = (f32[6,512,1280]{2,1,0:T(8,128)}, f32[6,512,1280]{2,1,0:T(8,128)}, u32[]{:S(2)}, u32[]{:S(2)}) collective-permute-start(f32[6,512,1280]{2,1,0:T(8,128)} %get-tuple-element.72), channel_id=1, source_target_pairs={{0,1},{1,0},{2,3},{3,2},{4,5},{5,4},{6,7},{7,6},{8,9},{9,8},{10,11... | collective-permute-start | bytes 47185928 | tf_op jit(solution)/shard_map/ppermute | solution.py:812
  549.3 46.5 %collective-permute-start.5 = (f32[4,512,1280]{2,1,0:T(8,128)}, f32[4,512,1280]{2,1,0:T(8,128)}, u32[]{:S(2)}, u32[]{:S(2)}) collective-permute-start(f32[4,512,1280]{2,1,0:T(8,128)} %get-tuple-element.73), channel_id=1, source_target_pairs={{0,1},{1,0},{2,3},{3,2},{4,5},{5,4},{6,7},{7,6},{8,9},{9,8},{10,11... | collective-permute-start | bytes 31457288 | tf_op jit(solution)/shard_map/ppermute | solution.py:812
  549.6 14.6 %collective-permute-start.3 = (f32[32,2048]{1,0:T(8,128)S(1)}, f32[32,2048]{1,0:T(8,128)S(1)}, u32[]{:S(2)}, u32[]{:S(2)}) collective-permute-start(f32[32,2048]{1,0:T(8,128)S(1)} %copy-done.8), channel_id=1, source_target_pairs={{0,8},{1,9},{2,10},{3,11},{4,12},{5,13},{6,14},{7,15},{8,0},{9,1},... | collective-permute-start | bytes 786440 | tf_op jit(solution)/shard_map/ppermute | solution.py:806
  617.1 6.5 copy-start
  631.6 30.9 %copy-start.5 = (f32[8,2048]{1,0:T(8,128)}, f32[8,2048]{1,0:T(8,128)S(1)}, u32[]{:S(2)}) copy-start(f32[8,2048]{1,0:T(8,128)S(1)} %bitcast_reduce_fusion) | copy-start | bytes 196612
  662.6 2.2 copy-start.1
  664.8 3.1 slice-start
Sparse Core Ops, SparseCore 0:
  90.3 42.6 all-gather.8
  135.7 47.2 all-gather.10
  320.8 85.2 all-gather.16
  408.1 184.9 all-gather.14
  595.3 35.3 all-gather.12

commit v5 on v3

--- a/solution.py
+++ b/solution.py
@@ -339,7 +339,7 @@
                 hq = slice(q * HB, q * HB + HB)
                 dout[t, :, :, hq] = groups_of(dext[:, hq] + dot(lowz, wt[:, hq]))
             state = (ne[0], ne[1], nd[0], nd[1])
-            us.append((rows_of(xin[k].astype(F32)), hin[k].astype(F32)))
+            us.append((rows_of(xin[k].astype(F32)).astype(BF16), hin[k]))
 
             @pl.when(t >= NR)
             def _():
@@ -348,7 +348,7 @@
 
         tcols = pl.ds(pl.multiple_of(lax.rem(p, CH // 2) * 2 * Q, 2 * Q), 2 * Q)
         for j in range(2):
-            ut[j * H:j * H + H, tcols] = jnp.concatenate([us[1][j], us[0][j]], axis=0).T.astype(BF16)
+            ut[j * H:j * H + H, tcols] = jnp.concatenate([us[1][j], us[0][j]], axis=0).T
 
         return state
 
@@ -456,11 +456,14 @@
         lse = top + jnp.log(tot)
         mx[rows, :] = jnp.broadcast_to(lse, (LANE, LANE))
         tb[rows, :] = jnp.broadcast_to(t_ref[rows, :], (LANE, LANE))
-        lane = lax.broadcasted_iota(jnp.int32, (LANE, LANE), 1)
-        stats_ref[rows, :] = jnp.where(lane < LANE // 2, mx[rows, :], tb[rows, :].astype(F32))
-
-    for r in range(0, N, LANE):
-        finish(r)
+
+    lane = lax.broadcasted_iota(jnp.int32, (LANE, LANE), 1)
+    stats = jnp.zeros((LANE, LANE), F32)
+    for j in range(N // LANE):
+        finish(j * LANE)
+        rows = slice(j * LANE, j * LANE + LANE)
+        stats = jnp.where(lane == j, mx[rows, :], jnp.where(lane == LANE - 1 - j, tb[rows, :].astype(F32), stats))
+    stats_ref[...] = stats
 
     def grads(b, gb, c):
         ids = [b * VB + c + h + lax.broadcasted_iota(jnp.int32, (RB, LANE), 1) for h in (0, LANE)]
@@ -504,7 +507,7 @@
 def head(x, tgt, w_vocab):
     return pl.pallas_call(
         head_kernel,
-        out_shape=(jax.ShapeDtypeStruct((N, H), F32), jax.ShapeDtypeStruct((N, LANE), F32)),
+        out_shape=(jax.ShapeDtypeStruct((N, H), F32), jax.ShapeDtypeStruct((LANE, LANE), F32)),
         in_specs=[VMEM, VMEM, ANY],
         out_specs=(VMEM, VMEM),
         scratch_shapes=[pltpu.VMEM((NVB, N, VB), F32), pltpu.VMEM((N, VB), BF16), pltpu.VMEM((N, VB), BF16), pltpu.VMEM((NW, H, VB), BF16),
@@ -611,8 +614,12 @@
         for c in range(0, TB, HB):
             rows = pl.ds(pl.multiple_of(k * TB + c, HB), HB)
             xtv[k, :, c:c + HB] = xv[rows, :].T
-            lse[rows, :] = jnp.broadcast_to(st_ref[rows, 0:1], (HB, LANE))
-            tgt[rows, :] = jnp.broadcast_to(st_ref[rows, LANE - 1:LANE], (HB, LANE))
+        for c in range(0, TB, LANE):
+            j = c % N // LANE
+            held = pl.ds(pl.multiple_of((k * (TB // N) + c // N) * LANE, LANE), LANE)
+            rows = pl.ds(pl.multiple_of(k * TB + c, LANE), LANE)
+            lse[rows, :] = jnp.broadcast_to(st_ref[held, j:j + 1], (LANE, LANE))
+            tgt[rows, :] = jnp.broadcast_to(st_ref[held, LANE - 1 - j:LANE - j], (LANE, LANE))
         return 0
 
     lax.fori_loop(0, NK, turn, 0)
@@ -744,7 +751,7 @@
         out_specs=HBM,
         input_output_aliases={1: 0} if len(args) > 1 else {},
         scratch_shapes=[pltpu.VMEM((NC,) + block, F32), DMA((NC,)), DMA((NC,))],
-        compiler_params=pltpu.CompilerParams(vmem_limit_bytes=24 * MIB),
+        compiler_params=pltpu.CompilerParams(vmem_limit_bytes=62 * MIB),
         cost_estimate=pl.CostEstimate(flops=20_000_000_000, bytes_accessed=130_000_000, transcendentals=0),
     )(*args)
 

time: 671 us -> 661 us (0.985)
  local copies, waits for them, and re-layouts: 12.4 us -> 4.31 us
    pallas_call x5, Pallas kernels: 61.5 us -> 70 us  [copy_call(): pl.pallas_call(kernel, out_shape=jax.ShapeDtypeStruct(out, F32), in_specs...]
    unnamed x20 -> x16, local copies, waits for them, and re-layouts: 11.5 us -> 3.42 us
    pallas_call x1, Pallas kernels: 129 us -> 121 us  [backward(): pl.pallas_call(bwd_kernel, out_shape=tuple((jax.ShapeDtypeStruct((rows, G...]
  transfers between devices with their start and end apart: 11 -> 11, of which waited for: 3 -> 3; matrix products, arithmetic and copies ran while one was open for 1% -> 1% of each run, Pallas kernels for 73% -> 74%
where the time goes in v5:
time: 661 us; the launch traced here: 659 us
  Pallas kernels  571 us (86%)
  waiting for transfers between devices  52.5 us (8%)
  between operations  14 us (2%)
  other arithmetic  11.9 us (2%)
    pallas_call x3, Pallas kernels, grad_vocab(): pl.pallas_call(functools.partial(dwv_kernel, lo, hi, counts), out_shape=o...  256 us
    pallas_call x1, Pallas kernels, backward(): pl.pallas_call(bwd_kernel, out_shape=tuple((jax.ShapeDtypeStruct((rows, G...  121 us
    pallas_call x1, Pallas kernels, forward(): pl.pallas_call(fwd_kernel, out_shape=(jax.ShapeDtypeStruct((T, Q, G4), F3...  80.8 us
    pallas_call x5, Pallas kernels, copy_call(): pl.pallas_call(kernel, out_shape=jax.ShapeDtypeStruct(out, F32), in_specs...  70 us
    pallas_call x1, Pallas kernels, head(): pl.pallas_call(head_kernel, out_shape=(jax.ShapeDtypeStruct((N, H), F32),...  43.1 us
    ppermute x3, waiting for transfers between devices, local_grads(): swapped.append((SPLITS[i], lax.ppermute(sent, 'data', other_core)))  40.1 us
  transfers between devices with their start and end apart: 11, of which 3 were waited for; matrix products, arithmetic and copies ran while one was open for 1% of the time, Pallas kernels for 74%

profile of v5, /device:TPU:0, one launch (start us, length us, event | category | flops | bytes accessed | tf_op | source)
XLA Modules:
  0.0 658.5 jit_solution(1120070064166941203)
XLA Ops:
  7.2 0.0 all-gather.9.cloned.1.call-start
  7.2 1.2 copy.27
  8.4 0.0 copy-start
  8.4 0.8 copy-done
  9.3 80.8 %lstm_fwd.1 = (f32[48,64,2048]{2,1,0:T(8,128)}, f32[48,64,512]{2,1,0:T(8,128)}, bf16[48,64,512]{2,1,0:T(8,128)(2,1)}, bf16[48,8,8,512]{3,2,1,0:T(8,128)(2,1)}, bf16[48,8,512]{2,1,0:T(8,128)(2,1)}) custom-call(bf16[48,8,512]{2,1,0:T(8,128)(2,1)S(1)} %bitcast.12, bf16[8,1024,2048]{2,1,0:T(8,128)(2,1)} %w_hbm.8, f32[8,2048]{1,0:T(8,128)S(1)} %copy-done), custom_call_target="tpu_custom_call" | custom-call | flops 60000002048 | bytes 80000000 | tf_op jit(solution)/shard_map/lstm_fwd/pallas_call | solution.py:196
  90.1 0.0 all-gather.9.cloned.1.call-update
  90.1 0.0 all-gather.11.cloned.1.call-start
  90.1 0.1 copy.23
  90.2 0.8 reshape.25.t_ref
  91.0 43.1 %head.1 = (f32[384,512]{1,0:T(8,128)}, f32[128,128]{1,0:T(8,128)}) custom-call(bf16[384,512]{1,0:T(8,128)(2,1)} %bitcast.1.x_ref, s32[384,1]{1,0:T(8,128)} %reshape.25.t_ref, bf16[512,32000]{1,0:T(8,128)(2,1)} %w_hbm.11), custom_call_target="tpu_custom_call" | custom-call | flops 40000000000 | bytes 70000000 | tf_op jit(solution)/shard_map/head/pallas_call | solution.py:508
  134.1 0.0 all-gather.11.cloned.1.call-update
  134.1 0.0 all-gather.17.cloned.1.call-start
  134.2 0.0 all-gather.9.cloned.1.call-done.x_hbm
  134.2 121.3 %lstm_bwd.1 = (f32[256,2048]{1,0:T(8,128)}, f32[352,2048]{1,0:T(8,128)}, f32[32,2048]{1,0:T(8,128)}, f32[352,2048]{1,0:T(8,128)}, f32[32,2048]{1,0:T(8,128)}, /*index=5*/f32[8,2048]{1,0:T(8,128)}, f32[48,8,512]{2,1,0:T(8,128)}) custom-call(f32[48,8,512]{2,1,0:T(8,128)} %bitcast.19, f32[48,64,2048]{2,1,0:T(8,128)} %get-tuple-element.43.gates_hbm, ...), custom_call_target="tpu_custom_call" | custom-call | flops 109999996928 | bytes 80000000 | tf_op jit(solution)/shard_map/lstm_bwd/pallas_call | solution.py:385
  255.5 1.4 collective-permute-start
  256.9 45.0 %dwv.3 = (f32[512,32000]{1,0:T(8,128)}, f32[2,512,1280]{2,1,0:T(8,128)}) custom-call(bf16[6144,512]{1,0:T(8,128)(2,1)} %all-gather.9.cloned.1.call-done.x_hbm, f32[2048,128]{1,0:T(8,128)} %all-gather.11.cloned.1.call-done.st_ref, bf16[512,32000]{1,0:T(8,128)(2,1)} %w_hbm.11), custom_call_target="tpu_custom_call" | custom-call | flops 40000000000 | bytes 100000000 | tf_op jit(solution)/shard_map/dwv/pallas_call | solution.py:696
  302.0 3.9 add.9
  305.9 0.0 all-gather.17.cloned.1.call-update
  305.9 0.0 all-gather.15.cloned.1.call-start
  306.0 0.9 collective-permute-start.1
  306.8 79.4 %dwv.4 = (f32[512,32000]{1,0:T(8,128)}, f32[4,512,1280]{2,1,0:T(8,128)}) custom-call(bf16[6144,512]{1,0:T(8,128)(2,1)} %all-gather.9.cloned.1.call-done.x_hbm, f32[2048,128]{1,0:T(8,128)} %all-gather.11.cloned.1.call-done.st_ref, bf16[512,32000]{1,0:T(8,128)(2,1)} %w_hbm.11, f32[512,32000]{1,0:T(8,128)} %get-tuple-element.55.rest_0_), custom_call_target="tpu_custom_call", output_to_operand_aliasing={{0}: (3, {})} | custom-call | flops 80000000000 | bytes 100000000 | tf_op jit(solution)/shard_map/dwv/pallas_call | solution.py:696
  386.3 3.2 add.10
  389.5 1.8 pad_maximum_fusion
  391.3 0.0 all-gather.15.cloned.1.call-update
  391.3 0.3 all-gather.13.cloned.1.call-start
  391.6 0.0 collective-permute-start.2
  391.7 9.7 %collective-permute-done.2.rest_1_ = f32[2,512,1280]{2,1,0:T(8,128)} collective-permute-done((f32[2,512,1280]{2,1,0:T(8,128)}, f32[2,512,1280]{2,1,0:T(8,128)}, u32[]{:S(2)}, u32[]{:S(2)}) %collective-permute-start.2) | collective-permute-done | bytes 5242912 | tf_op jit(solution)/shard_map/ppermute | solution.py:816
  401.4 131.9 %dwv.5 = (f32[512,32000]{1,0:T(8,128)}, f32[6,512,1280]{2,1,0:T(8,128)}) custom-call(bf16[6144,512]{1,0:T(8,128)(2,1)} %all-gather.9.cloned.1.call-done.x_hbm, f32[2048,128]{1,0:T(8,128)} %all-gather.11.cloned.1.call-done.st_ref, bf16[512,32000]{1,0:T(8,128)(2,1)} %w_hbm.11, ...), custom_call_target="tpu_custom_call", output_to_operand_aliasing={{0}: (3, {})} | custom-call | flops 140000002048 | bytes 100000000 | tf_op jit(solution)/shard_map/dwv/pallas_call | solution.py:696
  533.3 0.4 collective-permute-start.4
  533.7 0.2 collective-permute-start.5
  533.9 1.1 collective-permute-start.3
  534.9 1.3 copy.25
  536.3 12.2 %collective-permute-done.3 = f32[32,2048]{1,0:T(8,128)S(1)} collective-permute-done((f32[32,2048]{1,0:T(8,128)S(1)}, f32[32,2048]{1,0:T(8,128)S(1)}, u32[]{:S(2)}, u32[]{:S(2)}) %collective-permute-start.3) | collective-permute-done | bytes 262176 | tf_op jit(solution)/shard_map/ppermute | solution.py:810
  548.5 0.7 add.11
  549.2 0.0 all-gather.13.cloned.1.call-update
  549.3 30.3 %collective-permute-done.5.src = f32[4,512,1280]{2,1,0:T(8,128)} collective-permute-done((f32[4,512,1280]{2,1,0:T(8,128)}, f32[4,512,1280]{2,1,0:T(8,128)}, u32[]{:S(2)}, u32[]{:S(2)}) %collective-permute-start.5) | collective-permute-done | bytes 10485792 | tf_op jit(solution)/shard_map/ppermute | solution.py:816
  579.6 9.0 %shard_map.87._ = f32[512,32000]{1,0:T(8,128)} custom-call(f32[4,512,1280]{2,1,0:T(8,128)} %collective-permute-done.5.src, f32[512,32000]{1,0:T(8,128)} %get-tuple-element.74._), custom_call_target="tpu_custom_call", output_to_operand_aliasing={{}: (1, {})} | custom-call | flops 20000000000 | bytes 130000000 | tf_op jit(solution)/shard_map/pallas_call | solution.py:747
  588.6 12.2 %shard_map.88 = f32[512,32000]{1,0:T(8,128)} custom-call(f32[6,512,1280]{2,1,0:T(8,128)} %collective-permute-done.4.src, f32[512,32000]{1,0:T(8,128)} %shard_map.87._), custom_call_target="tpu_custom_call", output_to_operand_aliasing={{}: (1, {})} | custom-call | flops 20000000000 | bytes 130000000 | tf_op jit(solution)/shard_map/pallas_call | solution.py:747
  600.8 0.0 all-gather.17.cloned.1.call-done
  600.8 12.0 %shard_map.84.rest_0_ = f32[8,1024,2048]{2,1,0:T(8,128)} custom-call(f32[8,256,2048]{2,1,0:T(8,128)} %bitcast.15), custom_call_target="tpu_custom_call" | custom-call | flops 20000000000 | bytes 130000000 | tf_op jit(solution)/shard_map/pallas_call | solution.py:747
  612.8 0.0 all-gather.15.cloned.1.call-done
  612.8 1.6 slice_reduce_fusion
  614.4 0.0 copy-start.3
  614.5 31.0 %shard_map.85.rest_0_ = f32[8,1024,2048]{2,1,0:T(8,128)} custom-call(f32[16,360,2048]{2,1,0:T(8,128)} %bitcast.14, f32[8,1024,2048]{2,1,0:T(8,128)} %shard_map.84.rest_0_), custom_call_target="tpu_custom_call", output_to_operand_aliasing={{}: (1, {})} | custom-call | flops 20000000000 | bytes 130000000 | tf_op jit(solution)/shard_map/pallas_call | solution.py:747
  645.5 0.0 all-gather.13.cloned.1.call-done
  645.5 0.0 slice-start
  645.5 5.8 shard_map.86
  651.3 0.7 pad_maximum_fusion.1
  (18 shorter events, 0.1 us)
Async XLA Ops:
  7.2 127.0 %all-gather.9.cloned.1.call-start = ((), (), s32[]{:S(2)}) async-start(), calls=%async_computation | async-start | bytes 6684672 | tf_op jit(solution)/shard_map/all_gather | solution.py:799
  8.4 0.8 copy-start
  9.3 80.9 %copy-start.5 = (s32[8,48]{1,0:T(8,128)S(1)}, s32[8,48]{1,0:T(8,128)}, u32[]{:S(2)}) copy-start(s32[8,48]{1,0:T(8,128)} %param.6) | copy-start | bytes 4612
  90.1 166.9 %all-gather.11.cloned.1.call-start = ((), (), s32[]{:S(2)}) async-start(), calls=%async_computation.1 | async-start | bytes 1114112 | tf_op jit(solution)/shard_map/all_gather | solution.py:800
  134.1 466.7 %all-gather.17.cloned.1.call-start = ((), (), s32[]{:S(2)}) async-start(), calls=%async_computation.4 | async-start | bytes 18874368 | tf_op jit(solution)/shard_map/all_gather | solution.py:815
  255.5 46.5 %collective-permute-start = (f32[256,2048]{1,0:T(8,128)}, f32[256,2048]{1,0:T(8,128)}, u32[]{:S(2)}, u32[]{:S(2)}) collective-permute-start(f32[256,2048]{1,0:T(8,128)} %get-tuple-element.53), channel_id=1, source_target_pairs={{0,8},{1,9},{2,10},{3,11},{4,12},{5,13},{6,14},{7,15},{8,0},{9,1},... | collective-permute-start | bytes 6291464 | tf_op jit(solution)/shard_map/ppermute | solution.py:810
  305.9 306.9 %all-gather.15.cloned.1.call-start = ((), (), s32[]{:S(2)}) async-start(), calls=%async_computation.3 | async-start | bytes 50135040 | tf_op jit(solution)/shard_map/all_gather | solution.py:815
  306.0 80.3 %collective-permute-start.1 = (f32[352,2048]{1,0:T(8,128)}, f32[352,2048]{1,0:T(8,128)}, u32[]{:S(2)}, u32[]{:S(2)}) collective-permute-start(f32[352,2048]{1,0:T(8,128)} %get-tuple-element.60), channel_id=1, source_target_pairs={{0,8},{1,9},{2,10},{3,11},{4,12},{5,13},{6,14},{7,15},{8,0},{9,1},... | collective-permute-start | bytes 8650760 | tf_op jit(solution)/shard_map/ppermute | solution.py:810
  386.3 3.3 copy-start.4
  391.3 254.2 %all-gather.13.cloned.1.call-start = ((), (), s32[]{:S(2)}) async-start(), calls=%async_computation.2 | async-start | bytes 4456448 | tf_op jit(solution)/shard_map/all_gather | solution.py:815
  391.6 142.3 %copy-start.6 = (f32[32,2048]{1,0:T(8,128)S(1)}, f32[32,2048]{1,0:T(8,128)}, u32[]{:S(2)}) copy-start(f32[32,2048]{1,0:T(8,128)} %get-tuple-element.69) | copy-start | bytes 786436
  391.6 143.3 %copy-start.1 = (f32[48,8,512]{2,1,0:T(8,128)S(1)}, f32[48,8,512]{2,1,0:T(8,128)}, u32[]{:S(2)}) copy-start(f32[48,8,512]{2,1,0:T(8,128)} %get-tuple-element.75) | copy-start | bytes 2359300
  391.6 156.9 %copy-start.2 = (f32[32,2048]{1,0:T(8,128)S(1)}, f32[32,2048]{1,0:T(8,128)}, u32[]{:S(2)}) copy-start(f32[32,2048]{1,0:T(8,128)} %get-tuple-element.66) | copy-start | bytes 786436
  391.6 9.8 %collective-permute-start.2 = (f32[2,512,1280]{2,1,0:T(8,128)}, f32[2,512,1280]{2,1,0:T(8,128)}, u32[]{:S(2)}, u32[]{:S(2)}) collective-permute-start(f32[2,512,1280]{2,1,0:T(8,128)} %get-tuple-element.64), channel_id=1, source_target_pairs={{0,1},{1,0},{2,3},{3,2},{4,5},{5,4},{6,7},{7,6},{8,9},{9,8},{10,11... | collective-permute-start | bytes 15728648 | tf_op jit(solution)/shard_map/ppermute | solution.py:816
  533.3 55.3 %collective-permute-start.4 = (f32[6,512,1280]{2,1,0:T(8,128)}, f32[6,512,1280]{2,1,0:T(8,128)}, u32[]{:S(2)}, u32[]{:S(2)}) collective-permute-start(f32[6,512,1280]{2,1,0:T(8,128)} %get-tuple-element.72), channel_id=1, source_target_pairs={{0,1},{1,0},{2,3},{3,2},{4,5},{5,4},{6,7},{7,6},{8,9},{9,8},{10,11... | collective-permute-start | bytes 47185928 | tf_op jit(solution)/shard_map/ppermute | solution.py:816
  533.7 45.9 %collective-permute-start.5 = (f32[4,512,1280]{2,1,0:T(8,128)}, f32[4,512,1280]{2,1,0:T(8,128)}, u32[]{:S(2)}, u32[]{:S(2)}) collective-permute-start(f32[4,512,1280]{2,1,0:T(8,128)} %get-tuple-element.73), channel_id=1, source_target_pairs={{0,1},{1,0},{2,3},{3,2},{4,5},{5,4},{6,7},{7,6},{8,9},{9,8},{10,11... | collective-permute-start | bytes 31457288 | tf_op jit(solution)/shard_map/ppermute | solution.py:816
  533.9 14.6 %collective-permute-start.3 = (f32[32,2048]{1,0:T(8,128)S(1)}, f32[32,2048]{1,0:T(8,128)S(1)}, u32[]{:S(2)}, u32[]{:S(2)}) collective-permute-start(f32[32,2048]{1,0:T(8,128)S(1)} %copy-done.6), channel_id=1, source_target_pairs={{0,8},{1,9},{2,10},{3,11},{4,12},{5,13},{6,14},{7,15},{8,0},{9,1},... | collective-permute-start | bytes 786440 | tf_op jit(solution)/shard_map/ppermute | solution.py:810
  614.4 31.0 %copy-start.3 = (f32[8,2048]{1,0:T(8,128)}, f32[8,2048]{1,0:T(8,128)S(1)}, u32[]{:S(2)}) copy-start(f32[8,2048]{1,0:T(8,128)S(1)} %bitcast_reduce_fusion) | copy-start | bytes 196612
  645.5 5.8 slice-start
Sparse Core Ops, SparseCore 0:
  90.2 42.9 all-gather.8
  136.0 36.2 all-gather.10
  306.0 89.3 all-gather.16
  397.5 183.3 all-gather.14
  583.0 36.4 all-gather.12

commit v6 on v5

--- a/solution.py
+++ b/solution.py
@@ -709,48 +709,52 @@
     )(x_all, stats, w_vocab, *before, *(v for _, v in came))
 
 
-NC = 8
+RING = 24 * MIB
 
 
 def copy_ring(n, src, dst, buf, isem, osem):
+    nbuf = buf.shape[0]
+    ahead = nbuf // 2
+
     def fetch(i):
-        k = lax.rem(i, NC)
+        k = lax.rem(i, nbuf)
         return pltpu.make_async_copy(src(i), buf.at[k], isem.at[k])
 
     def put(i):
-        k = lax.rem(i, NC)
+        k = lax.rem(i, nbuf)
         return pltpu.make_async_copy(buf.at[k], dst(i), osem.at[k])
 
-    for i in range(NC // 2):
+    for i in range(min(ahead, n)):
         fetch(i).start()
 
     def body(i, _):
         fetch(i).wait()
         put(i).start()
 
-        @pl.when(i >= NC // 2)
-        def _():
-            put(i - NC // 2).wait()
-
-        @pl.when(i + NC // 2 < n)
-        def _():
-            fetch(i + NC // 2).start()
+        @pl.when(i >= ahead)
+        def _():
+            put(i - ahead).wait()
+
+        @pl.when(i + ahead < n)
+        def _():
+            fetch(i + ahead).start()
 
         return 0
 
     lax.fori_loop(0, n, body, 0)
-    for i in range(n - NC // 2, n):
+    for i in range(max(n - ahead, 0), n):
         put(i).wait()
 
 
 def copy_call(kernel, out, block, args):
+    nbuf = min(RING // (block[0] * block[1] * 4), 2 * NDEV)
     return pl.pallas_call(
         kernel,
         out_shape=jax.ShapeDtypeStruct(out, F32),
         in_specs=[HBM] * len(args),
         out_specs=HBM,
         input_output_aliases={1: 0} if len(args) > 1 else {},
-        scratch_shapes=[pltpu.VMEM((NC,) + block, F32), DMA((NC,)), DMA((NC,))],
+        scratch_shapes=[pltpu.VMEM((nbuf,) + block, F32), DMA((nbuf,)), DMA((nbuf,))],
         compiler_params=pltpu.CompilerParams(vmem_limit_bytes=62 * MIB),
         cost_estimate=pl.CostEstimate(flops=20_000_000_000, bytes_accessed=130_000_000, transcendentals=0),
     )(*args)

time: 661 us -> 658 us (level)
  no operation moved by 1% of the time
where the time goes in v6:
time: 658 us; the launch traced here: 656 us
  Pallas kernels  569 us (86%)
  waiting for transfers between devices  52.5 us (8%)
  between operations  14 us (2%)
  other arithmetic  11.8 us (2%)
    pallas_call x3, Pallas kernels, grad_vocab(): pl.pallas_call(functools.partial(dwv_kernel, lo, hi, counts), out_shape=o...  256 us
    pallas_call x1, Pallas kernels, backward(): pl.pallas_call(bwd_kernel, out_shape=tuple((jax.ShapeDtypeStruct((rows, G...  121 us
    pallas_call x1, Pallas kernels, forward(): pl.pallas_call(fwd_kernel, out_shape=(jax.ShapeDtypeStruct((T, Q, G4), F3...  80.8 us
    pallas_call x5, Pallas kernels, copy_call(): pl.pallas_call(kernel, out_shape=jax.ShapeDtypeStruct(out, F32), in_specs...  67.4 us
    pallas_call x1, Pallas kernels, head(): pl.pallas_call(head_kernel, out_shape=(jax.ShapeDtypeStruct((N, H), F32),...  43.1 us
    ppermute x3, waiting for transfers between devices, local_grads(): swapped.append((SPLITS[i], lax.ppermute(sent, 'data', other_core)))  40.1 us
  transfers between devices with their start and end apart: 11, of which 3 were waited for; matrix products, arithmetic and copies ran while one was open for 1% of the time, Pallas kernels for 74%

profile of v6, /device:TPU:0, one launch (start us, length us, event | category | flops | bytes accessed | tf_op | source)
XLA Modules:
  0.0 655.9 jit_solution(9541023673030254238)
XLA Ops:
  7.2 0.0 all-gather.9.cloned.1.call-start
  7.2 1.2 copy.27
  8.4 0.0 copy-start
  8.4 0.8 copy-done
  9.3 80.8 %lstm_fwd.1 = (f32[48,64,2048]{2,1,0:T(8,128)}, f32[48,64,512]{2,1,0:T(8,128)}, bf16[48,64,512]{2,1,0:T(8,128)(2,1)}, bf16[48,8,8,512]{3,2,1,0:T(8,128)(2,1)}, bf16[48,8,512]{2,1,0:T(8,128)(2,1)}) custom-call(bf16[48,8,512]{2,1,0:T(8,128)(2,1)S(1)} %bitcast.12, bf16[8,1024,2048]{2,1,0:T(8,128)(2,1)} %w_hbm.8, f32[8,2048]{1,0:T(8,128)S(1)} %copy-done), custom_call_target="tpu_custom_call" | custom-call | flops 60000002048 | bytes 80000000 | tf_op jit(solution)/shard_map/lstm_fwd/pallas_call | solution.py:196
  90.1 0.0 all-gather.9.cloned.1.call-update
  90.1 0.0 all-gather.11.cloned.1.call-start
  90.1 0.1 copy.23
  90.2 0.8 reshape.25.t_ref
  91.0 43.1 %head.1 = (f32[384,512]{1,0:T(8,128)}, f32[128,128]{1,0:T(8,128)}) custom-call(bf16[384,512]{1,0:T(8,128)(2,1)} %bitcast.1.x_ref, s32[384,1]{1,0:T(8,128)} %reshape.25.t_ref, bf16[512,32000]{1,0:T(8,128)(2,1)} %w_hbm.11), custom_call_target="tpu_custom_call" | custom-call | flops 40000000000 | bytes 70000000 | tf_op jit(solution)/shard_map/head/pallas_call | solution.py:508
  134.1 0.0 all-gather.11.cloned.1.call-update
  134.1 0.0 all-gather.17.cloned.1.call-start
  134.2 0.0 all-gather.9.cloned.1.call-done.x_hbm
  134.2 121.3 %lstm_bwd.1 = (f32[256,2048]{1,0:T(8,128)}, f32[352,2048]{1,0:T(8,128)}, f32[32,2048]{1,0:T(8,128)}, f32[352,2048]{1,0:T(8,128)}, f32[32,2048]{1,0:T(8,128)}, /*index=5*/f32[8,2048]{1,0:T(8,128)}, f32[48,8,512]{2,1,0:T(8,128)}) custom-call(f32[48,8,512]{2,1,0:T(8,128)} %bitcast.19, f32[48,64,2048]{2,1,0:T(8,128)} %get-tuple-element.43.gates_hbm, ...), custom_call_target="tpu_custom_call" | custom-call | flops 109999996928 | bytes 80000000 | tf_op jit(solution)/shard_map/lstm_bwd/pallas_call | solution.py:385
  255.5 1.4 collective-permute-start
  256.9 45.0 %dwv.3 = (f32[512,32000]{1,0:T(8,128)}, f32[2,512,1280]{2,1,0:T(8,128)}) custom-call(bf16[6144,512]{1,0:T(8,128)(2,1)} %all-gather.9.cloned.1.call-done.x_hbm, f32[2048,128]{1,0:T(8,128)} %all-gather.11.cloned.1.call-done.st_ref, bf16[512,32000]{1,0:T(8,128)(2,1)} %w_hbm.11), custom_call_target="tpu_custom_call" | custom-call | flops 40000000000 | bytes 100000000 | tf_op jit(solution)/shard_map/dwv/pallas_call | solution.py:696
  302.0 3.9 add.9
  305.9 0.0 all-gather.17.cloned.1.call-update
  305.9 0.0 all-gather.15.cloned.1.call-start
  306.0 0.9 collective-permute-start.1
  306.8 79.4 %dwv.4 = (f32[512,32000]{1,0:T(8,128)}, f32[4,512,1280]{2,1,0:T(8,128)}) custom-call(bf16[6144,512]{1,0:T(8,128)(2,1)} %all-gather.9.cloned.1.call-done.x_hbm, f32[2048,128]{1,0:T(8,128)} %all-gather.11.cloned.1.call-done.st_ref, bf16[512,32000]{1,0:T(8,128)(2,1)} %w_hbm.11, f32[512,32000]{1,0:T(8,128)} %get-tuple-element.55.rest_0_), custom_call_target="tpu_custom_call", output_to_operand_aliasing={{0}: (3, {})} | custom-call | flops 80000000000 | bytes 100000000 | tf_op jit(solution)/shard_map/dwv/pallas_call | solution.py:696
  386.3 3.2 add.10
  389.5 1.8 pad_maximum_fusion
  391.3 0.0 all-gather.15.cloned.1.call-update
  391.3 0.3 all-gather.13.cloned.1.call-start
  391.6 0.0 collective-permute-start.2
  391.7 9.7 %collective-permute-done.2.rest_1_ = f32[2,512,1280]{2,1,0:T(8,128)} collective-permute-done((f32[2,512,1280]{2,1,0:T(8,128)}, f32[2,512,1280]{2,1,0:T(8,128)}, u32[]{:S(2)}, u32[]{:S(2)}) %collective-permute-start.2) | collective-permute-done | bytes 5242912 | tf_op jit(solution)/shard_map/ppermute | solution.py:820
  401.4 131.9 %dwv.5 = (f32[512,32000]{1,0:T(8,128)}, f32[6,512,1280]{2,1,0:T(8,128)}) custom-call(bf16[6144,512]{1,0:T(8,128)(2,1)} %all-gather.9.cloned.1.call-done.x_hbm, f32[2048,128]{1,0:T(8,128)} %all-gather.11.cloned.1.call-done.st_ref, bf16[512,32000]{1,0:T(8,128)(2,1)} %w_hbm.11, ...), custom_call_target="tpu_custom_call", output_to_operand_aliasing={{0}: (3, {})} | custom-call | flops 140000002048 | bytes 100000000 | tf_op jit(solution)/shard_map/dwv/pallas_call | solution.py:696
  533.3 0.4 collective-permute-start.4
  533.7 0.2 collective-permute-start.5
  533.9 1.1 collective-permute-start.3
  534.9 1.3 copy.25
  536.3 12.2 %collective-permute-done.3 = f32[32,2048]{1,0:T(8,128)S(1)} collective-permute-done((f32[32,2048]{1,0:T(8,128)S(1)}, f32[32,2048]{1,0:T(8,128)S(1)}, u32[]{:S(2)}, u32[]{:S(2)}) %collective-permute-start.3) | collective-permute-done | bytes 262176 | tf_op jit(solution)/shard_map/ppermute | solution.py:814
  548.5 0.7 add.11
  549.2 0.0 all-gather.13.cloned.1.call-update
  549.3 30.3 %collective-permute-done.5.src = f32[4,512,1280]{2,1,0:T(8,128)} collective-permute-done((f32[4,512,1280]{2,1,0:T(8,128)}, f32[4,512,1280]{2,1,0:T(8,128)}, u32[]{:S(2)}, u32[]{:S(2)}) %collective-permute-start.5) | collective-permute-done | bytes 10485792 | tf_op jit(solution)/shard_map/ppermute | solution.py:820
  579.6 8.3 %shard_map.87._ = f32[512,32000]{1,0:T(8,128)} custom-call(f32[4,512,1280]{2,1,0:T(8,128)} %collective-permute-done.5.src, f32[512,32000]{1,0:T(8,128)} %get-tuple-element.74._), custom_call_target="tpu_custom_call", output_to_operand_aliasing={{}: (1, {})} | custom-call | flops 20000000000 | bytes 130000000 | tf_op jit(solution)/shard_map/pallas_call | solution.py:751
  588.0 11.7 %shard_map.88 = f32[512,32000]{1,0:T(8,128)} custom-call(f32[6,512,1280]{2,1,0:T(8,128)} %collective-permute-done.4.src, f32[512,32000]{1,0:T(8,128)} %shard_map.87._), custom_call_target="tpu_custom_call", output_to_operand_aliasing={{}: (1, {})} | custom-call | flops 20000000000 | bytes 130000000 | tf_op jit(solution)/shard_map/pallas_call | solution.py:751
  599.7 0.0 all-gather.17.cloned.1.call-done
  599.7 12.1 %shard_map.84.rest_0_ = f32[8,1024,2048]{2,1,0:T(8,128)} custom-call(f32[8,256,2048]{2,1,0:T(8,128)} %bitcast.15), custom_call_target="tpu_custom_call" | custom-call | flops 20000000000 | bytes 130000000 | tf_op jit(solution)/shard_map/pallas_call | solution.py:751
  611.8 0.0 all-gather.15.cloned.1.call-done
  611.8 1.5 slice_reduce_fusion
  613.4 0.0 copy-start.3
  613.4 31.1 %shard_map.85.rest_0_ = f32[8,1024,2048]{2,1,0:T(8,128)} custom-call(f32[16,360,2048]{2,1,0:T(8,128)} %bitcast.14, f32[8,1024,2048]{2,1,0:T(8,128)} %shard_map.84.rest_0_), custom_call_target="tpu_custom_call", output_to_operand_aliasing={{}: (1, {})} | custom-call | flops 20000000000 | bytes 130000000 | tf_op jit(solution)/shard_map/pallas_call | solution.py:751
  644.5 0.0 all-gather.13.cloned.1.call-done
  644.5 0.0 slice-start
  644.5 4.1 shard_map.86
  648.7 0.7 pad_maximum_fusion.1
  (18 shorter events, 0.1 us)
Async XLA Ops:
  7.2 127.0 %all-gather.9.cloned.1.call-start = ((), (), s32[]{:S(2)}) async-start(), calls=%async_computation | async-start | bytes 6684672 | tf_op jit(solution)/shard_map/all_gather | solution.py:803
  8.4 0.8 copy-start
  9.3 80.9 %copy-start.5 = (s32[8,48]{1,0:T(8,128)S(1)}, s32[8,48]{1,0:T(8,128)}, u32[]{:S(2)}) copy-start(s32[8,48]{1,0:T(8,128)} %param.6) | copy-start | bytes 4612
  90.1 166.9 %all-gather.11.cloned.1.call-start = ((), (), s32[]{:S(2)}) async-start(), calls=%async_computation.1 | async-start | bytes 1114112 | tf_op jit(solution)/shard_map/all_gather | solution.py:804
  134.1 465.6 %all-gather.17.cloned.1.call-start = ((), (), s32[]{:S(2)}) async-start(), calls=%async_computation.4 | async-start | bytes 18874368 | tf_op jit(solution)/shard_map/all_gather | solution.py:819
  255.5 46.5 %collective-permute-start = (f32[256,2048]{1,0:T(8,128)}, f32[256,2048]{1,0:T(8,128)}, u32[]{:S(2)}, u32[]{:S(2)}) collective-permute-start(f32[256,2048]{1,0:T(8,128)} %get-tuple-element.53), channel_id=1, source_target_pairs={{0,8},{1,9},{2,10},{3,11},{4,12},{5,13},{6,14},{7,15},{8,0},{9,1},... | collective-permute-start | bytes 6291464 | tf_op jit(solution)/shard_map/ppermute | solution.py:814
  305.9 305.9 %all-gather.15.cloned.1.call-start = ((), (), s32[]{:S(2)}) async-start(), calls=%async_computation.3 | async-start | bytes 50135040 | tf_op jit(solution)/shard_map/all_gather | solution.py:819
  306.0 80.3 %collective-permute-start.1 = (f32[352,2048]{1,0:T(8,128)}, f32[352,2048]{1,0:T(8,128)}, u32[]{:S(2)}, u32[]{:S(2)}) collective-permute-start(f32[352,2048]{1,0:T(8,128)} %get-tuple-element.60), channel_id=1, source_target_pairs={{0,8},{1,9},{2,10},{3,11},{4,12},{5,13},{6,14},{7,15},{8,0},{9,1},... | collective-permute-start | bytes 8650760 | tf_op jit(solution)/shard_map/ppermute | solution.py:814
  386.3 3.3 copy-start.4
  391.3 253.2 %all-gather.13.cloned.1.call-start = ((), (), s32[]{:S(2)}) async-start(), calls=%async_computation.2 | async-start | bytes 4456448 | tf_op jit(solution)/shard_map/all_gather | solution.py:819
  391.6 142.3 %copy-start.6 = (f32[32,2048]{1,0:T(8,128)S(1)}, f32[32,2048]{1,0:T(8,128)}, u32[]{:S(2)}) copy-start(f32[32,2048]{1,0:T(8,128)} %get-tuple-element.69) | copy-start | bytes 786436
  391.6 143.3 %copy-start.1 = (f32[48,8,512]{2,1,0:T(8,128)S(1)}, f32[48,8,512]{2,1,0:T(8,128)}, u32[]{:S(2)}) copy-start(f32[48,8,512]{2,1,0:T(8,128)} %get-tuple-element.75) | copy-start | bytes 2359300
  391.6 156.9 %copy-start.2 = (f32[32,2048]{1,0:T(8,128)S(1)}, f32[32,2048]{1,0:T(8,128)}, u32[]{:S(2)}) copy-start(f32[32,2048]{1,0:T(8,128)} %get-tuple-element.66) | copy-start | bytes 786436
  391.6 9.8 %collective-permute-start.2 = (f32[2,512,1280]{2,1,0:T(8,128)}, f32[2,512,1280]{2,1,0:T(8,128)}, u32[]{:S(2)}, u32[]{:S(2)}) collective-permute-start(f32[2,512,1280]{2,1,0:T(8,128)} %get-tuple-element.64), channel_id=1, source_target_pairs={{0,1},{1,0},{2,3},{3,2},{4,5},{5,4},{6,7},{7,6},{8,9},{9,8},{10,11... | collective-permute-start | bytes 15728648 | tf_op jit(solution)/shard_map/ppermute | solution.py:820
  533.3 54.6 %collective-permute-start.4 = (f32[6,512,1280]{2,1,0:T(8,128)}, f32[6,512,1280]{2,1,0:T(8,128)}, u32[]{:S(2)}, u32[]{:S(2)}) collective-permute-start(f32[6,512,1280]{2,1,0:T(8,128)} %get-tuple-element.72), channel_id=1, source_target_pairs={{0,1},{1,0},{2,3},{3,2},{4,5},{5,4},{6,7},{7,6},{8,9},{9,8},{10,11... | collective-permute-start | bytes 47185928 | tf_op jit(solution)/shard_map/ppermute | solution.py:820
  533.7 45.9 %collective-permute-start.5 = (f32[4,512,1280]{2,1,0:T(8,128)}, f32[4,512,1280]{2,1,0:T(8,128)}, u32[]{:S(2)}, u32[]{:S(2)}) collective-permute-start(f32[4,512,1280]{2,1,0:T(8,128)} %get-tuple-element.73), channel_id=1, source_target_pairs={{0,1},{1,0},{2,3},{3,2},{4,5},{5,4},{6,7},{7,6},{8,9},{9,8},{10,11... | collective-permute-start | bytes 31457288 | tf_op jit(solution)/shard_map/ppermute | solution.py:820
  533.9 14.6 %collective-permute-start.3 = (f32[32,2048]{1,0:T(8,128)S(1)}, f32[32,2048]{1,0:T(8,128)S(1)}, u32[]{:S(2)}, u32[]{:S(2)}) collective-permute-start(f32[32,2048]{1,0:T(8,128)S(1)} %copy-done.6), channel_id=1, source_target_pairs={{0,8},{1,9},{2,10},{3,11},{4,12},{5,13},{6,14},{7,15},{8,0},{9,1},... | collective-permute-start | bytes 786440 | tf_op jit(solution)/shard_map/ppermute | solution.py:814
  613.4 31.1 %copy-start.3 = (f32[8,2048]{1,0:T(8,128)}, f32[8,2048]{1,0:T(8,128)S(1)}, u32[]{:S(2)}) copy-start(f32[8,2048]{1,0:T(8,128)S(1)} %bitcast_reduce_fusion) | copy-start | bytes 196612
  644.5 4.2 slice-start
Sparse Core Ops, SparseCore 0:
  90.2 42.9 all-gather.8
  136.0 36.2 all-gather.10
  306.0 89.3 all-gather.16
  397.5 183.3 all-gather.14
  583.0 36.4 all-gather.12
